TPU v7x, 32 devices: a whole 2x2x4 slice. The times are simulated.
32 devices in a mesh: groups: 2 (over x), seq: 16 (over z, y, core).
Axes of the slice: x: 2, y: 2, z: 4, core: 2. Of those that a mesh axis runs over, the one named last changes fastest.
Arguments:
- hidden: bfloat16 [1024, 3072], P(('groups', 'seq')), parts along dimension 0, may hold values from -6 to 6
- queries: bfloat16 [1024, 3072], P(('groups', 'seq')), parts along dimension 0, may hold values from -6 to 6
- key_rows: bfloat16 [1024, 3072], P(('groups', 'seq')), parts along dimension 0, may hold values from -6 to 6
- values: bfloat16 [1024, 3072], P(('groups', 'seq')), parts along dimension 0, may hold values from -12 to 12
- query_gain: float32 [2, 128], replicated, may hold values from 0.6 to 5
- key_gain: float32 [2, 128], replicated, may hold values from 0.6 to 5
- gate_table: bfloat16 [8, 2, 3072], P('groups'), parts along dimension 0, may hold values from -6 to 6
- segment: int32 [1024], P(('groups', 'seq')), parts along dimension 0, may hold values from 0 to 3, as said below
- text_count: int32 [8], P('groups'), parts along dimension 0, may hold values from 1 to 40
Outputs:
- mixed: bfloat16 [1024, 3072], P(('groups', 'seq')), parts along dimension 0
There are 2 independent parts, one for each index of `groups`. A program takes and returns all parts, laid end to end along the dimension named above; an argument that names none is the same for every part. Nothing has to cross between parts.
Inputs may be any that keep to these rules, and one draw needn't show every extreme that they name: `segment`: one device holds at most 10 tokens of one request; in every draw some two requests 2 j and 2 j + 1 get exactly 10 tokens from every device. Tokens of one request may lie anywhere on the devices.
All inputs are finite; a program needn't handle non-finite values.
Results may differ from a plain program's by a relative error of at most 0.012.
The roundings to bfloat16 on the way count: a program that leaves them out, or rounds other values in their place, can miss the bound.
Values may be sent and summed in bfloat16 or wider, within the bound.
A program may use at most 64 MiB of HBM per device.

v0:
```python
import functools
import math

import jax
import jax.numpy as jnp
from jax import lax
from jax.experimental import pallas as pl
from jax.experimental.pallas import tpu as pltpu
from jax.sharding import PartitionSpec as P

HEAD_DIM = 128


EPSILON = 1e-06
MASKED = -1e30


def head_norm(rows_in, gains, stream):
    row_count = rows_in.shape[0]
    per_head = rows_in.astype(jnp.float32).reshape(row_count, -1, HEAD_DIM)
    inverse = lax.rsqrt(jnp.mean(per_head * per_head, axis=-1, keepdims=True) + EPSILON)
    gain_rows = jnp.where((stream == 0)[:, None], gains[0][None, :], gains[1][None, :])
    return (per_head * inverse * gain_rows[:, None, :]).astype(jnp.bfloat16).reshape(row_count, -1)


def attend(query_block, block_segment, key_data, value_data, key_segment):
    scores = jnp.einsum(
        "qhd,khd->hqk", query_block, key_data, preferred_element_type=jnp.float32
    ) * (1.0 / math.sqrt(HEAD_DIM))
    allowed = (block_segment[:, None] == key_segment[None, :])[None, :, :]
    scores = jnp.where(allowed, scores, MASKED)
    largest = jnp.max(scores, axis=-1, keepdims=True)
    weights = jnp.exp(scores - largest)
    weights = (weights / jnp.sum(weights, axis=-1, keepdims=True)).astype(jnp.bfloat16)
    return jnp.einsum(
        "hqk,khd->qhd", weights, value_data, preferred_element_type=jnp.float32
    ).astype(jnp.bfloat16)


def per_device(
    hidden, queries, key_rows, values, query_gain, key_gain, gate_table, segment, text_count
):
    tok_rows = hidden.shape[0]
    width_all = hidden.shape[1]
    devices = lax.axis_size("seq")
    requests = text_count.shape[0]
    seg_hot = (segment[:, None] == jnp.arange(requests, dtype=jnp.int32)[None, :]).astype(jnp.int32)
    local_counts = jnp.sum(seg_hot, axis=0)
    all_counts = lax.all_gather(local_counts[None, :], "seq", axis=0, tiled=True)
    lower_rows = (jnp.arange(devices, dtype=jnp.int32) < lax.axis_index("seq")).astype(jnp.int32)
    before = jnp.sum(all_counts * lower_rows[:, None], axis=0)
    position = jnp.sum((jnp.cumsum(seg_hot, axis=0) - seg_hot + before[None, :]) * seg_hot, axis=1)
    text_limit = jnp.sum(seg_hot * text_count[None, :], axis=1)
    stream = (position >= text_limit).astype(jnp.int32)
    query_normed = head_norm(queries, query_gain, stream)
    key_normed = head_norm(key_rows, key_gain, stream)
    groups = 8
    pair_merge = 2
    slices = devices // groups
    cap_rows = 4 * tok_rows // devices + max(1, tok_rows // devices)
    bucket_rows = cap_rows * pair_merge
    head_cols = width_all // groups
    owner_slice = segment // pair_merge
    owner_hot = (owner_slice[:, None] == jnp.arange(slices, dtype=jnp.int32)[None, :]).astype(
        jnp.int32
    )
    owner_rank = jnp.sum((jnp.cumsum(owner_hot, axis=0) - owner_hot) * owner_hot, axis=1)
    slot_place = owner_slice * bucket_rows + owner_rank
    bucket_index = (
        jnp.full((slices * bucket_rows,), tok_rows, jnp.int32)
        .at[slot_place]
        .set(jnp.arange(tok_rows, dtype=jnp.int32))
    )
    stacked = jnp.concatenate(
        [
            query_normed.reshape(tok_rows, groups, head_cols),
            key_normed.reshape(tok_rows, groups, head_cols),
            values.reshape(tok_rows, groups, head_cols),
        ],
        axis=2,
    ).transpose(1, 0, 2)
    outgoing = jnp.take(stacked, bucket_index, axis=1, mode="fill", fill_value=0).reshape(
        devices, bucket_rows, 3 * head_cols
    )
    slot_segment = jnp.take(segment, bucket_index, axis=0, mode="fill", fill_value=-1)
    segment_out = jnp.broadcast_to(slot_segment[None, :], (groups, slices * bucket_rows)).reshape(
        devices, bucket_rows
    )
    arrived, arrived_segment = (
        lax.all_to_all(outgoing, "seq", split_axis=0, concat_axis=0, tiled=True),
        lax.all_to_all(segment_out, "seq", split_axis=0, concat_axis=0, tiled=True),
    )
    slot_count = devices * bucket_rows
    per_head = head_cols // HEAD_DIM
    slot_data = arrived.reshape(slot_count, 3 * head_cols)
    query_all = slot_data[:, :head_cols].reshape(slot_count, per_head, HEAD_DIM)
    key_all = slot_data[:, head_cols : 2 * head_cols].reshape(slot_count, per_head, HEAD_DIM)
    value_all = slot_data[:, 2 * head_cols :].reshape(slot_count, per_head, HEAD_DIM)
    key_segment = arrived_segment.reshape(slot_count)
    if slot_count % 512 == 0:
        block_rows = 512
    elif slot_count % 256 == 0:
        block_rows = 256
    else:
        block_rows = slot_count

    def one_block(first_row):
        return attend(query_all, key_segment, key_all, value_all, key_segment)

    results = lax.map(one_block, jnp.arange(slot_count // block_rows, dtype=jnp.int32) * block_rows)
    returning = results.reshape(devices, bucket_rows, head_cols)
    returned = lax.all_to_all(returning, "seq", split_axis=0, concat_axis=0, tiled=True)
    returned = returned.reshape(groups, slices * bucket_rows, head_cols)
    attention = (
        jnp.take(returned, slot_place, axis=1).transpose(1, 0, 2).reshape(tok_rows, width_all)
    )
    gate_rows = jnp.take(gate_table.reshape(requests * 2, width_all), segment * 2 + stream, axis=0)
    mixed = hidden.astype(jnp.float32) + gate_rows.astype(jnp.float32) * attention.astype(
        jnp.float32
    )
    return mixed.astype(jnp.bfloat16)


LANES = 128
CONTRACT_LAST = (((1,), (1,)), ((), ()))


def normed(rows, gain_rows):
    wide = rows.astype(jnp.float32)
    inverse = lax.rsqrt(jnp.mean(wide * wide, axis=-1, keepdims=True) + EPSILON)
    return (wide * inverse * gain_rows).astype(jnp.bfloat16)


def fused_kernel(
    devices, requests, segment_hbm, query_hbm, key_hbm, value_hbm,
    text_hbm, hidden_hbm, query_gain_hbm, key_gain_hbm, gate_hbm, out_hbm,
    text_ref, hidden_ref, query_gain_ref, key_gain_ref, gate_ref, out_ref,
    stage, recv, query_n, key_n, result, back, seg_all, hot, text, bias, gate_rows,
    stage_sem, own_sem, seg_own_sem, load_sem, store_sem, seg_send, seg_recv,
    out_send, out_recv, relay_send, relay_recv, back_send, back_recv,
):
    chips = devices // 2
    tok = hidden_hbm.shape[0]
    per_chip = hidden_hbm.shape[1] // HEAD_DIM // chips
    tokens = devices * tok
    mine = chips * tok
    me = lax.axis_index("seq")
    chip, core = me // 2, me % 2
    partner = me + 1 - 2 * core
    sources = (query_hbm, key_hbm, value_hbm)

    def columns(head):
        return pl.ds(pl.multiple_of(head * HEAD_DIM, HEAD_DIM), HEAD_DIM)

    def remote(src, dst, send_sem, recv_sem, device):
        return pltpu.make_async_remote_copy(
            src_ref=src, dst_ref=dst, send_sem=send_sem, recv_sem=recv_sem,
            device_id={"seq": device}, device_id_type=pl.DeviceIdType.MESH,
        )

    barrier = pltpu.get_barrier_semaphore()
    for device in [(chip + step) % chips * 2 + core for step in range(1, chips)] + [partner]:
        pl.semaphore_signal(
            barrier, inc=1, device_id={"seq": device},
            device_id_type=pl.DeviceIdType.MESH,
        )
    seg_own = pltpu.make_async_copy(segment_hbm, seg_all.at[me], seg_own_sem)
    seg_own.start()
    for head in range(per_chip):
        for step in range(1, chips):
            target = (chip + step) % chips
            for part, source in enumerate(sources):
                pltpu.make_async_copy(
                    source.at[:, columns(target * per_chip + head)],
                    stage.at[head, step - 1, part],
                    stage_sem.at[head],
                ).start()
        for part, source in enumerate(sources):
            pltpu.make_async_copy(
                source.at[:, columns(chip * per_chip + head)],
                recv.at[head, me, part],
                own_sem.at[head],
            ).start()
    loads = [
        pltpu.make_async_copy(source, target, load_sem.at[place])
        for place, (source, target) in enumerate(
            (
                (text_hbm, text_ref), (query_gain_hbm, query_gain_ref),
                (key_gain_hbm, key_gain_ref), (gate_hbm, gate_ref), (hidden_hbm, hidden_ref),
            )
        )
    ]
    for copy in loads:
        copy.start()
    seg_own.wait()
    pl.semaphore_wait(barrier, chips)

    seg_copies = []
    seg_relays = []

    def send_ids(source, kind, step, device):
        copy = remote(
            seg_all.at[source], seg_all.at[source],
            seg_send.at[kind, step], seg_recv.at[kind, step], device,
        )
        copy.start()
        return copy

    for step in range(chips - 1, 0, -1):
        seg_copies.insert(0, send_ids(me, 0, step, (chip + step) % chips * 2 + core))
    seg_relays.append(send_ids(me, 1, 0, partner))
    out_copies = []
    for head in range(per_chip):
        pltpu.make_async_copy(stage.at[head], stage.at[head], stage_sem.at[head]).wait()
        row = []
        for step in range(chips - 1, 0, -1):
            copy = remote(
                stage.at[head, step - 1], recv.at[head, me],
                out_send.at[head, step - 1], out_recv.at[head, step - 1],
                (chip + step) % chips * 2 + core,
            )
            copy.start()
            row.insert(0, copy)
        out_copies.append(row)

    relay_copies = []

    def relay(head, step, source):
        copy = remote(
            recv.at[head, source, pl.ds(1, 2)], recv.at[head, source, pl.ds(1, 2)],
            relay_send.at[head, step], relay_recv.at[head, step], partner,
        )
        copy.start()
        return copy

    for head in range(per_chip):
        pltpu.make_async_copy(
            recv.at[head, me], recv.at[head, me], own_sem.at[head]
        ).wait()
        relay_copies.append([relay(head, 0, me)])

    for step in range(1, chips):
        seg_copies[step - 1].wait_recv()
        source = (chip + chips - step) % chips * 2 + core
        seg_relays.append(send_ids(source, 1, step, partner))
    for copy in seg_relays:
        copy.wait_recv()
    for copy in loads:
        copy.wait()
    eye = (
        lax.broadcasted_iota(jnp.int32, (tok, tok), 0)
        == lax.broadcasted_iota(jnp.int32, (tok, tok), 1)
    ).astype(jnp.float32).astype(jnp.bfloat16)
    ids = lax.broadcasted_iota(jnp.int32, (LANES, tok), 0)
    for n in range(devices):
        flipped = (ids == seg_all[n]).astype(jnp.float32).astype(jnp.bfloat16)
        hot[n] = lax.dot_general(
            eye, flipped, CONTRACT_LAST, preferred_element_type=jnp.float32
        ).astype(jnp.bfloat16)
    all_hot = hot[...].reshape(tokens, LANES)
    earlier = (
        lax.broadcasted_iota(jnp.int32, (tokens, tokens), 1)
        < lax.broadcasted_iota(jnp.int32, (tokens, tokens), 0)
    ).astype(jnp.float32).astype(jnp.bfloat16)
    before = jnp.dot(earlier, all_hot, preferred_element_type=jnp.float32)
    lane = lax.broadcasted_iota(jnp.int32, (1, LANES), 1)
    limit = jnp.zeros((1, LANES), jnp.int32)
    for r in range(requests):
        limit = jnp.where(lane == r, text_ref[0:1, r : r + 1], limit)
    inside = jnp.where(before < limit.astype(jnp.float32), all_hot.astype(jnp.float32), 0.0)
    ones = jnp.ones((LANES, LANES), jnp.bfloat16)
    text[...] = jnp.dot(
        inside.astype(jnp.bfloat16), ones, preferred_element_type=jnp.float32
    ).reshape(devices, tok, LANES)
    for c in range(chips):
        same = lax.dot_general(
            hot[2 * c + core], all_hot, CONTRACT_LAST, preferred_element_type=jnp.float32
        )
        bias[c * tok : (c + 1) * tok] = jnp.where(same > 0.5, 0.0, MASKED)

    number = lax.broadcasted_iota(jnp.int32, (LANES, LANES), 0).astype(jnp.float32)
    own_id = jnp.dot(
        hot[me], number.astype(jnp.bfloat16), preferred_element_type=jnp.float32
    )
    own_code = 2.0 * own_id + jnp.where(text[me] > 0.5, 0.0, 1.0)
    for tile in range(hidden_ref.shape[1] // LANES):
        cols = slice(tile * LANES, (tile + 1) * LANES)
        total = jnp.zeros((tok, LANES), jnp.float32)
        for r in range(requests):
            pair = gate_ref[r, :, cols].astype(jnp.float32)
            for s in range(2):
                total = jnp.where(own_code == float(2 * r + s), pair[s : s + 1], total)
        gate_rows[tile] = total

    query_gain, key_gain = query_gain_ref[...], key_gain_ref[...]

    def gain_of(gain, n):
        return jnp.where(text[n] > 0.5, gain[0:1], gain[1:2])

    scale = 1.0 / math.sqrt(HEAD_DIM)
    back_copies = []
    for head in range(per_chip):
        for step in range(1, chips):
            out_copies[head][step - 1].wait_recv()
            source = (chip + chips - step) % chips * 2 + core
            relay_copies[head].append(relay(head, step, source))
        for c in range(chips):
            n = 2 * c + core
            query_n[c] = normed(recv[head, n, 0], gain_of(query_gain, n))
            key_n[n] = normed(recv[head, n, 1], gain_of(key_gain, n))
        for step in range(chips):
            relay_copies[head][step].wait_recv()
            n = (chip + chips - step) % chips * 2 + 1 - core
            key_n[n] = normed(recv[head, n, 1], gain_of(key_gain, n))
        keys = key_n[...].reshape(tokens, HEAD_DIM)
        vals = recv[head, :, 2].reshape(tokens, HEAD_DIM)
        scores = lax.dot_general(
            query_n[...].reshape(mine, HEAD_DIM), keys, CONTRACT_LAST,
            preferred_element_type=jnp.float32,
        ) * scale + bias[...]
        largest = jnp.max(scores, axis=-1, keepdims=True)
        weights = jnp.exp(scores - largest)
        weights = (weights / jnp.sum(weights, axis=-1, keepdims=True)).astype(jnp.bfloat16)
        result[head] = jnp.dot(
            weights, vals, preferred_element_type=jnp.float32
        ).astype(jnp.bfloat16).reshape(chips, tok, HEAD_DIM)
        row = []
        for step in range(1, chips):
            target = (chip + step) % chips
            copy = remote(
                result.at[head, target], back.at[chip * per_chip + head],
                back_send.at[head, step - 1], back_recv.at[head, step - 1],
                target * 2 + core,
            )
            copy.start()
            row.append(copy)
        back_copies.append(row)

    def finish(index, attention):
        out_ref[:, columns(index)] = (
            hidden_ref[:, columns(index)].astype(jnp.float32)
            + gate_rows[index] * attention.astype(jnp.float32)
        ).astype(jnp.bfloat16)
        pltpu.make_async_copy(
            out_ref.at[:, columns(index)], out_hbm.at[:, columns(index)], store_sem
        ).start()

    for head in range(per_chip):
        finish(chip * per_chip + head, result[head, chip])
        for step in range(1, chips):
            back_copies[head][step - 1].wait_recv()
            index = (chip + chips - step) % chips * per_chip + head
            finish(index, back[index])
    for copy in seg_copies + seg_relays:
        copy.wait_send()
    for rows in (out_copies, relay_copies, back_copies):
        for row in rows:
            for copy in row:
                copy.wait_send()
    pltpu.make_async_copy(out_ref, out_hbm, store_sem).wait()


def fused(
    hidden, queries, key_rows, values, query_gain, key_gain, gate_table, segment, text_count
):
    devices = lax.axis_size("seq")
    chips = devices // 2
    tok, width = hidden.shape
    heads = width // HEAD_DIM
    per_chip = heads // chips
    hbm = pl.BlockSpec(memory_space=pl.ANY)
    block = (tok, HEAD_DIM)
    dma = pltpu.SemaphoreType.DMA
    return pl.pallas_call(
        functools.partial(fused_kernel, devices, text_count.shape[0]),
        out_shape=jax.ShapeDtypeStruct((tok, width), jnp.bfloat16),
        in_specs=[hbm] * 9,
        out_specs=hbm,
        scratch_shapes=[
            pltpu.VMEM((1, text_count.shape[0]), jnp.int32),
            pltpu.VMEM(hidden.shape, hidden.dtype),
            pltpu.VMEM(query_gain.shape, query_gain.dtype),
            pltpu.VMEM(key_gain.shape, key_gain.dtype),
            pltpu.VMEM(gate_table.shape, gate_table.dtype),
            pltpu.VMEM(hidden.shape, jnp.bfloat16),
            pltpu.VMEM((per_chip, chips - 1, 3) + block, jnp.bfloat16),
            pltpu.VMEM((per_chip, devices, 3) + block, jnp.bfloat16),
            pltpu.VMEM((chips,) + block, jnp.bfloat16),
            pltpu.VMEM((devices,) + block, jnp.bfloat16),
            pltpu.VMEM((per_chip, chips) + block, jnp.bfloat16),
            pltpu.VMEM((heads,) + block, jnp.bfloat16),
            pltpu.VMEM((devices, 1, tok), jnp.int32),
            pltpu.VMEM((devices, tok, LANES), jnp.bfloat16),
            pltpu.VMEM((devices, tok, LANES), jnp.float32),
            pltpu.VMEM((chips * tok, devices * tok), jnp.float32),
            pltpu.VMEM((heads, tok, LANES), jnp.float32),
            dma((per_chip,)),
            dma((per_chip,)),
            dma,
            dma((5,)),
            dma,
            dma((2, chips)),
            dma((2, chips)),
            dma((per_chip, chips - 1)),
            dma((per_chip, chips - 1)),
            dma((per_chip, chips)),
            dma((per_chip, chips)),
            dma((per_chip, chips - 1)),
            dma((per_chip, chips - 1)),
        ],
        compiler_params=pltpu.CompilerParams(collective_id=0, has_side_effects=True),
    )(
        segment.reshape(1, tok), queries, key_rows, values,
        text_count.reshape(1, -1), hidden, query_gain, key_gain, gate_table,
    )


def program(*arrays):
    devices = lax.axis_size("seq")
    tok, width = arrays[0].shape
    requests = arrays[-1].shape[0]
    whole_heads = devices % 2 == 0 and (width // HEAD_DIM) % (devices // 2) == 0
    if whole_heads and devices * tok <= 1024 and requests <= LANES and tok % 16 == 0:
        return fused(*arrays)
    return per_device(*arrays)


def solution(mesh):
    return jax.shard_map(
        program,
        mesh=mesh,
        in_specs=(
            P(("groups", "seq"), None),
            P(("groups", "seq"), None),
            P(("groups", "seq"), None),
            P(("groups", "seq"), None),
            P(),
            P(),
            P("groups", None, None),
            P(("groups", "seq")),
            P("groups"),
        ),
        out_specs=P(("groups", "seq"), None),
        check_vma=False,
    )
```

profile of v0, /device:TPU:0, one launch (start us, length us, event | category | flops | bytes accessed | tf_op | source)
XLA Modules:
  0.0 30.6 jit_solution(12232211894047056378)
XLA Ops:
  0.0 29.0 %shard_map.91 = bf16[32,3072]{1,0:T(8,128)(2,1)} custom-call(s32[1,32]{1,0:T(1,128)} %bitcast.2, bf16[32,3072]{1,0:T(8,128)(2,1)} %query_hbm.1, bf16[32,3072]{1,0:T(8,128)(2,1)} %key_hbm.1, bf16[32,3072]{1,0:T(8,128)(2,1)} %value_hbm.1, s32[1,4]{1,0:T(1,128)} %bitcast.3, bf16[32,3072]{1,0:T(8,128)(2,1)} %hidden_hbm.1, f32[2,128]{1,0:T(2,128)} %query_gain_hbm.1, ...), custom_call_target="tpu_custom_call" | custom-call | tf_op jit(solution)/shard_map/pallas_call | solution.py:374
  29.0 1.6 %copy.11 = bf16[32,3072]{1,0:T(8,128)(2,1)} copy(bf16[32,3072]{1,0:T(8,128)(2,1)} %shard_map.91) | data formatting | bytes 393216
where the time goes:
time: 30.8 us; the launch traced here: 30.6 us
  Pallas kernels  29 us (94%)
  local copies, waits for them, and re-layouts  1.62 us (5%)
    pallas_call x1, Pallas kernels, fused(): pl.pallas_call(functools.partial(fused_kernel, devices, text_count.shape[...  29 us
    unnamed x1, local copies, waits for them, and re-layouts  1.62 us

commit v1 on v0

v1 whole, which is shorter than its diff:
```python
import functools
import math

import jax
import jax.numpy as jnp
from jax import lax
from jax.experimental import pallas as pl
from jax.experimental.pallas import tpu as pltpu
from jax.sharding import PartitionSpec as P

HEAD_DIM = 128


EPSILON = 1e-06
MASKED = -1e30


def head_norm(rows_in, gains, stream):
    row_count = rows_in.shape[0]
    per_head = rows_in.astype(jnp.float32).reshape(row_count, -1, HEAD_DIM)
    inverse = lax.rsqrt(jnp.mean(per_head * per_head, axis=-1, keepdims=True) + EPSILON)
    gain_rows = jnp.where((stream == 0)[:, None], gains[0][None, :], gains[1][None, :])
    return (per_head * inverse * gain_rows[:, None, :]).astype(jnp.bfloat16).reshape(row_count, -1)


def attend(query_block, block_segment, key_data, value_data, key_segment):
    scores = jnp.einsum(
        "qhd,khd->hqk", query_block, key_data, preferred_element_type=jnp.float32
    ) * (1.0 / math.sqrt(HEAD_DIM))
    allowed = (block_segment[:, None] == key_segment[None, :])[None, :, :]
    scores = jnp.where(allowed, scores, MASKED)
    largest = jnp.max(scores, axis=-1, keepdims=True)
    weights = jnp.exp(scores - largest)
    weights = (weights / jnp.sum(weights, axis=-1, keepdims=True)).astype(jnp.bfloat16)
    return jnp.einsum(
        "hqk,khd->qhd", weights, value_data, preferred_element_type=jnp.float32
    ).astype(jnp.bfloat16)


def per_device(
    hidden, queries, key_rows, values, query_gain, key_gain, gate_table, segment, text_count
):
    tok_rows = hidden.shape[0]
    width_all = hidden.shape[1]
    devices = lax.axis_size("seq")
    requests = text_count.shape[0]
    seg_hot = (segment[:, None] == jnp.arange(requests, dtype=jnp.int32)[None, :]).astype(jnp.int32)
    local_counts = jnp.sum(seg_hot, axis=0)
    all_counts = lax.all_gather(local_counts[None, :], "seq", axis=0, tiled=True)
    lower_rows = (jnp.arange(devices, dtype=jnp.int32) < lax.axis_index("seq")).astype(jnp.int32)
    before = jnp.sum(all_counts * lower_rows[:, None], axis=0)
    position = jnp.sum((jnp.cumsum(seg_hot, axis=0) - seg_hot + before[None, :]) * seg_hot, axis=1)
    text_limit = jnp.sum(seg_hot * text_count[None, :], axis=1)
    stream = (position >= text_limit).astype(jnp.int32)
    query_normed = head_norm(queries, query_gain, stream)
    key_normed = head_norm(key_rows, key_gain, stream)
    groups = 8
    pair_merge = 2
    slices = devices // groups
    cap_rows = 4 * tok_rows // devices + max(1, tok_rows // devices)
    bucket_rows = cap_rows * pair_merge
    head_cols = width_all // groups
    owner_slice = segment // pair_merge
    owner_hot = (owner_slice[:, None] == jnp.arange(slices, dtype=jnp.int32)[None, :]).astype(
        jnp.int32
    )
    owner_rank = jnp.sum((jnp.cumsum(owner_hot, axis=0) - owner_hot) * owner_hot, axis=1)
    slot_place = owner_slice * bucket_rows + owner_rank
    bucket_index = (
        jnp.full((slices * bucket_rows,), tok_rows, jnp.int32)
        .at[slot_place]
        .set(jnp.arange(tok_rows, dtype=jnp.int32))
    )
    stacked = jnp.concatenate(
        [
            query_normed.reshape(tok_rows, groups, head_cols),
            key_normed.reshape(tok_rows, groups, head_cols),
            values.reshape(tok_rows, groups, head_cols),
        ],
        axis=2,
    ).transpose(1, 0, 2)
    outgoing = jnp.take(stacked, bucket_index, axis=1, mode="fill", fill_value=0).reshape(
        devices, bucket_rows, 3 * head_cols
    )
    slot_segment = jnp.take(segment, bucket_index, axis=0, mode="fill", fill_value=-1)
    segment_out = jnp.broadcast_to(slot_segment[None, :], (groups, slices * bucket_rows)).reshape(
        devices, bucket_rows
    )
    arrived, arrived_segment = (
        lax.all_to_all(outgoing, "seq", split_axis=0, concat_axis=0, tiled=True),
        lax.all_to_all(segment_out, "seq", split_axis=0, concat_axis=0, tiled=True),
    )
    slot_count = devices * bucket_rows
    per_head = head_cols // HEAD_DIM
    slot_data = arrived.reshape(slot_count, 3 * head_cols)
    query_all = slot_data[:, :head_cols].reshape(slot_count, per_head, HEAD_DIM)
    key_all = slot_data[:, head_cols : 2 * head_cols].reshape(slot_count, per_head, HEAD_DIM)
    value_all = slot_data[:, 2 * head_cols :].reshape(slot_count, per_head, HEAD_DIM)
    key_segment = arrived_segment.reshape(slot_count)
    if slot_count % 512 == 0:
        block_rows = 512
    elif slot_count % 256 == 0:
        block_rows = 256
    else:
        block_rows = slot_count

    def one_block(first_row):
        return attend(query_all, key_segment, key_all, value_all, key_segment)

    results = lax.map(one_block, jnp.arange(slot_count // block_rows, dtype=jnp.int32) * block_rows)
    returning = results.reshape(devices, bucket_rows, head_cols)
    returned = lax.all_to_all(returning, "seq", split_axis=0, concat_axis=0, tiled=True)
    returned = returned.reshape(groups, slices * bucket_rows, head_cols)
    attention = (
        jnp.take(returned, slot_place, axis=1).transpose(1, 0, 2).reshape(tok_rows, width_all)
    )
    gate_rows = jnp.take(gate_table.reshape(requests * 2, width_all), segment * 2 + stream, axis=0)
    mixed = hidden.astype(jnp.float32) + gate_rows.astype(jnp.float32) * attention.astype(
        jnp.float32
    )
    return mixed.astype(jnp.bfloat16)


LANES = 128
CONTRACT_LAST = (((1,), (1,)), ((), ()))


def normed(rows, gain_rows):
    wide = rows.astype(jnp.float32)
    inverse = lax.rsqrt(jnp.mean(wide * wide, axis=-1, keepdims=True) + EPSILON)
    return (wide * inverse * gain_rows).astype(jnp.bfloat16)


def fused_kernel(
    devices, segment_hbm, query_hbm, key_hbm, value_hbm,
    text_hbm, hidden_hbm, query_gain_hbm, key_gain_hbm, gate_hbm, out_ref,
    text_ref, hidden_ref, query_gain_ref, key_gain_ref, gate_ref,
    staged, shared, owned, weights, shared_out, owned_out, back, seg_all, hot, earlier,
    query_gains, key_gains, bias, gate_rows,
    level_sem, row_sem, across_sem, core_sem, pair_sem,
    load_sem, seg_own_sem, stage_sem, slot_sem,
    seg_send, seg_recv, send_sem, recv_sem, relay_send, relay_recv,
):
    chips = devices // 2
    levels = chips // 2
    tok = hidden_hbm.shape[0]
    per_chip = hidden_hbm.shape[1] // HEAD_DIM // chips
    own_heads = per_chip // 2
    requests = gate_hbm.shape[0]
    tokens = devices * tok
    me = lax.axis_index("seq")
    chip, core = me // 2, me % 2
    row, level = chip % 2, chip // 2
    partner = me + 1 - 2 * core
    sources = (query_hbm, key_hbm, value_hbm)

    def columns(head):
        return pl.ds(pl.multiple_of(head * HEAD_DIM, HEAD_DIM), HEAD_DIM)

    def chip_at(a_level, a_row):
        return a_level * 2 + a_row

    def signal(semaphore, device):
        pl.semaphore_signal(
            semaphore, inc=1, device_id={"seq": device}, device_id_type=pl.DeviceIdType.MESH
        )

    def remote(src, dst, send, recv, device):
        copy = pltpu.make_async_remote_copy(
            src_ref=src, dst_ref=dst, send_sem=send, recv_sem=recv,
            device_id={"seq": device}, device_id_type=pl.DeviceIdType.MESH,
        )
        copy.start()
        return copy

    def settle(ref, semaphore):
        pltpu.make_async_copy(ref, ref, semaphore).wait()

    toward = 1 - 2 * (level // (levels // 2))
    near_first = [(level + levels + toward * step) % levels for step in range(1, levels)]
    far_first = [(level + levels - toward * step) % levels for step in range(1, levels)]

    barrier = pltpu.get_barrier_semaphore()
    for step in range(1, levels):
        @pl.when(level + step < levels)
        def _():
            signal(barrier, chip_at(level + step, row) * 2 + core)

    @pl.when(row == 0)
    def _():
        signal(barrier, chip_at(level, 1) * 2 + core)

    @pl.when(core == 0)
    def _():
        signal(barrier, partner)

    seg_own = pltpu.make_async_copy(segment_hbm, seg_all.at[chip, core], seg_own_sem)
    seg_own.start()
    for part, source in enumerate(sources):
        pltpu.make_async_copy(source, staged.at[part], stage_sem.at[part // 2]).start()
    for part, source in enumerate(sources):
        pltpu.make_async_copy(
            source.at[:, columns(chip * per_chip)], shared.at[part, chip, core], slot_sem.at[0]
        ).start()
        for j in range(own_heads):
            pltpu.make_async_copy(
                source.at[:, columns(chip * per_chip + 1 + core * own_heads + j)],
                owned.at[j, part, chip, core], slot_sem.at[1 + j],
            ).start()
    loads = [
        pltpu.make_async_copy(source, target, load_sem.at[place])
        for place, (source, target) in enumerate(
            (
                (text_hbm, text_ref), (query_gain_hbm, query_gain_ref),
                (key_gain_hbm, key_gain_ref), (gate_hbm, gate_ref), (hidden_hbm, hidden_ref),
            )
        )
    ]
    for copy in loads:
        copy.start()
    seg_own.wait()
    settle(staged.at[0:2], stage_sem.at[0])

    @pl.when(me > 0)
    def _():
        pl.semaphore_wait(barrier, level + row + core)

    for step in range(1, levels):
        @pl.when(level >= step)
        def _():
            signal(level_sem.at[level], chip_at(level - step, row) * 2 + core)

    @pl.when(row == 1)
    def _():
        signal(row_sem, chip_at(level, 0) * 2 + core)

    @pl.when(core == 1)
    def _():
        signal(core_sem, partner)

    seg_copies = []

    def send_shared(to_chip):
        seg_copies.append(remote(
            seg_all.at[chip, core], seg_all.at[chip, core],
            seg_send.at[len(seg_copies)], seg_recv.at[chip], to_chip * 2 + core,
        ))
        remote(
            staged.at[0:2, :, columns(to_chip * per_chip)], shared.at[0:2, chip, core],
            send_sem.at[0], recv_sem.at[0], to_chip * 2 + core,
        )

    def meet(a_level):
        @pl.when(a_level > level)
        def _():
            pl.semaphore_wait(level_sem.at[a_level], 1)

    meet(near_first[0])
    send_shared(chip_at(near_first[0], row))

    @pl.when(row == 0)
    def _():
        pl.semaphore_wait(row_sem, 1)

    signal(across_sem.at[level], chip_at(near_first[0], row) * 2 + core)
    send_shared(chip_at(level, 1 - row))
    for a_level in near_first[1:]:
        meet(a_level)
        signal(across_sem.at[level], chip_at(a_level, row) * 2 + core)
        send_shared(chip_at(a_level, row))
    for a_level in near_first:
        pl.semaphore_wait(across_sem.at[a_level], 1)
        send_shared(chip_at(a_level, 1 - row))

    near_chips = [chip_at(a, row) for a in near_first] + [chip_at(level, 1 - row)]
    near_chips += [chip_at(a, 1 - row) for a in near_first]
    far_chips = [chip_at(a, 1 - row) for a in far_first] + [chip_at(a, row) for a in far_first]
    far_chips += [chip_at(level, 1 - row)]

    settle(staged.at[2], stage_sem.at[1])
    for to_chip in near_chips:
        remote(
            staged.at[2, :, columns(to_chip * per_chip)], shared.at[2, chip, core],
            send_sem.at[1], recv_sem.at[1], to_chip * 2 + core,
        )

    @pl.when(core == 0)
    def _():
        pl.semaphore_wait(core_sem, 1)

    for to_chip in near_chips:
        signal(pair_sem, to_chip * 2 + core)

    def own_head(j, a_core):
        return 1 + a_core * own_heads + j

    beside = [
        remote(
            staged.at[:, :, columns(chip * per_chip + own_head(j, 1 - core))],
            owned.at[j, :, chip, core], relay_send.at[3 + j], relay_recv.at[3 + j], partner,
        )
        for j in range(own_heads)
    ]

    earlier[...] = (
        lax.broadcasted_iota(jnp.int32, (tokens, tokens), 1)
        < lax.broadcasted_iota(jnp.int32, (tokens, tokens), 0)
    ).astype(jnp.float32).astype(jnp.bfloat16)

    pl.semaphore_wait(pair_sem, chips - 1)
    for j in range(own_heads):
        for to_chip in near_chips:
            for a_core in range(2):
                remote(
                    staged.at[0:2, :, columns(to_chip * per_chip + own_head(j, a_core))],
                    owned.at[j, 0:2, chip, core],
                    send_sem.at[4 + 2 * j], recv_sem.at[4 + 2 * j], to_chip * 2 + a_core,
                )
    for j in range(own_heads):
        for to_chip in far_chips:
            for a_core in range(2):
                remote(
                    staged.at[2, :, columns(to_chip * per_chip + own_head(j, a_core))],
                    owned.at[j, 2, chip, core],
                    send_sem.at[5 + 2 * j], recv_sem.at[5 + 2 * j], to_chip * 2 + a_core,
                )

    for step in range(1, chips):
        source = (chip + step) % chips
        settle(seg_all.at[source, core], seg_recv.at[source])
    seg_relay = remote(
        seg_all.at[:, core], seg_all.at[:, core], relay_send.at[0], relay_recv.at[0], partner
    )
    for copy in loads:
        copy.wait()
    seg_relay.wait_recv()
    eye = (
        lax.broadcasted_iota(jnp.int32, (tok, tok), 0)
        == lax.broadcasted_iota(jnp.int32, (tok, tok), 1)
    ).astype(jnp.float32).astype(jnp.bfloat16)
    ids = lax.broadcasted_iota(jnp.int32, (LANES, tok), 0)
    for n in range(devices):
        flipped = (ids == seg_all[n // 2, n % 2]).astype(jnp.float32).astype(jnp.bfloat16)
        hot[n] = lax.dot_general(
            eye, flipped, CONTRACT_LAST, preferred_element_type=jnp.float32
        ).astype(jnp.bfloat16)
    all_hot = hot[...].reshape(tokens, LANES)
    before = jnp.dot(earlier[...], all_hot, preferred_element_type=jnp.float32)
    lane = lax.broadcasted_iota(jnp.int32, (1, LANES), 1)
    limit = jnp.zeros((1, LANES), jnp.int32)
    for r in range(requests):
        limit = jnp.where(lane == r, text_ref[0:1, r : r + 1], limit)
    inside = jnp.where(before < limit.astype(jnp.float32), all_hot.astype(jnp.float32), 0.0)
    text = jnp.dot(
        inside.astype(jnp.bfloat16), jnp.ones((LANES, LANES), jnp.bfloat16),
        preferred_element_type=jnp.float32,
    ) > 0.5
    query_gain, key_gain = query_gain_ref[...], key_gain_ref[...]
    spread = (chips, 2, tok, LANES)
    query_gains[...] = jnp.where(text, query_gain[0:1], query_gain[1:2]).reshape(spread)
    key_gains[...] = jnp.where(text, key_gain[0:1], key_gain[1:2]).reshape(spread)
    same = lax.dot_general(all_hot, all_hot, CONTRACT_LAST, preferred_element_type=jnp.float32)
    bias[...] = jnp.where(same > 0.5, 0.0, MASKED).reshape(chips, 2, tok, tokens)

    scale = 1.0 / math.sqrt(HEAD_DIM)

    def attention_weights(query_n, key_n, query_bias):
        scores = lax.dot_general(
            query_n, key_n, CONTRACT_LAST, preferred_element_type=jnp.float32
        ) * scale + query_bias
        grown = jnp.exp(scores - jnp.max(scores, axis=-1, keepdims=True))
        return (grown * (1.0 / jnp.sum(grown, axis=-1, keepdims=True))).astype(jnp.bfloat16)

    settle(shared.at[:, chip, core], slot_sem.at[0])
    settle(shared.at[0:2, 0 : chips - 1, 0], recv_sem.at[0])
    relays = [remote(
        shared.at[1, :, core], shared.at[1, :, core], relay_send.at[1], relay_recv.at[1], partner
    )]
    settle(shared.at[2, 0 : chips - 1, 0], recv_sem.at[1])
    relays.append(remote(
        shared.at[2, :, core], shared.at[2, :, core], relay_send.at[2], relay_recv.at[2], partner
    ))
    half = (tokens // 2, HEAD_DIM)
    full = (tokens, HEAD_DIM)
    query_n = normed(shared.at[0, :, core][...], query_gains.at[:, core][...]).reshape(half)
    relays[0].wait_recv()
    key_n = normed(shared[1], key_gains[...]).reshape(full)
    part_weights = attention_weights(
        query_n, key_n, bias.at[:, core][...].reshape(tokens // 2, tokens)
    )
    relays[1].wait_recv()
    shared_out[...] = jnp.dot(
        part_weights, shared[2].reshape(full), preferred_element_type=jnp.float32
    ).astype(jnp.bfloat16).reshape(chips, tok, HEAD_DIM)
    for to_chip in far_chips:
        remote(
            shared_out.at[to_chip], back.at[chip * per_chip],
            send_sem.at[2], recv_sem.at[2], to_chip * 2 + core,
        )

    number = lax.broadcasted_iota(jnp.int32, (LANES, LANES), 0).astype(jnp.float32)
    own_id = jnp.dot(hot[me], number.astype(jnp.bfloat16), preferred_element_type=jnp.float32)
    own_before = jnp.dot(
        earlier[pl.ds(pl.multiple_of(me * tok, tok), tok), :], all_hot,
        preferred_element_type=jnp.float32,
    )
    own_inside = jnp.where(
        own_before < limit.astype(jnp.float32), hot[me].astype(jnp.float32), 0.0
    )
    own_text = jnp.dot(
        own_inside.astype(jnp.bfloat16), jnp.ones((LANES, LANES), jnp.bfloat16),
        preferred_element_type=jnp.float32,
    )
    own_code = 2.0 * own_id + jnp.where(own_text > 0.5, 0.0, 1.0)
    for tile in range(hidden_ref.shape[1] // LANES):
        cols = slice(tile * LANES, (tile + 1) * LANES)
        total = jnp.zeros((tok, LANES), jnp.float32)
        for r in range(requests):
            pair = gate_ref[r, :, cols].astype(jnp.float32)
            for s in range(2):
                total = jnp.where(own_code == float(2 * r + s), pair[s : s + 1], total)
        gate_rows[tile] = total

    for j in range(own_heads):
        settle(owned.at[j, :, chip, core], slot_sem.at[1 + j])
        settle(owned.at[j, 0:2, 0 : chips - 1], recv_sem.at[4 + 2 * j])
        beside[j].wait_recv()
        query_n = normed(owned[j, 0], query_gains[...]).reshape(full)
        key_n = normed(owned[j, 1], key_gains[...]).reshape(full)
        weights[j] = attention_weights(query_n, key_n, bias[...].reshape(tokens, tokens))
    for j in range(own_heads):
        settle(owned.at[j, 2, 0 : chips - 1], recv_sem.at[5 + 2 * j])
        owned_out[j] = jnp.dot(
            weights[j], owned[j, 2].reshape(full), preferred_element_type=jnp.float32
        ).astype(jnp.bfloat16).reshape(chips, 2, tok, HEAD_DIM)
        head = chip * per_chip + own_head(j, core)
        for to_chip in far_chips:
            for a_core in range(2):
                remote(
                    owned_out.at[j, to_chip, a_core], back.at[head],
                    send_sem.at[3], recv_sem.at[3], to_chip * 2 + a_core,
                )
        remote(
            owned_out.at[j, chip, 1 - core], back.at[head],
            send_sem.at[3], recv_sem.at[3], partner,
        )

    def finish(head):
        cols = slice(head * HEAD_DIM, (head + 1) * HEAD_DIM)
        out_ref[:, cols] = (
            hidden_ref[:, cols].astype(jnp.float32)
            + gate_rows[head] * back[head].astype(jnp.float32)
        ).astype(jnp.bfloat16)

    back[chip * per_chip] = shared_out[chip]
    settle(back.at[0 : chips - 1], recv_sem.at[2])
    for a_chip in range(chips):
        finish(a_chip * per_chip)
    for j in range(own_heads):
        back[chip * per_chip + own_head(j, core)] = owned_out.at[j, chip, core][...]
    settle(back.at[0 : own_heads * (devices - 1)], recv_sem.at[3])
    for a_chip in range(chips):
        for head in range(1, per_chip):
            finish(a_chip * per_chip + head)

    for copy in seg_copies + [seg_relay] + relays + beside:
        copy.wait_send()
    settle(shared.at[0:2, 0 : chips - 1, 0], send_sem.at[0])
    settle(shared.at[2, 0 : chips - 1, 0], send_sem.at[1])
    settle(back.at[0 : chips - 1], send_sem.at[2])
    settle(back.at[0 : own_heads * (devices - 1)], send_sem.at[3])
    for j in range(own_heads):
        settle(owned.at[j, 0:2, 0 : chips - 1], send_sem.at[4 + 2 * j])
        settle(owned.at[j, 2, 0 : chips - 1], send_sem.at[5 + 2 * j])


def fused(
    hidden, queries, key_rows, values, query_gain, key_gain, gate_table, segment, text_count
):
    devices = lax.axis_size("seq")
    chips = devices // 2
    levels = chips // 2
    tok, width = hidden.shape
    heads = width // HEAD_DIM
    own_heads = heads // chips // 2
    tokens = devices * tok
    hbm = pl.BlockSpec(memory_space=pl.ANY)
    block = (tok, HEAD_DIM)
    dma = pltpu.SemaphoreType.DMA
    regular = pltpu.SemaphoreType.REGULAR
    return pl.pallas_call(
        functools.partial(fused_kernel, devices),
        out_shape=jax.ShapeDtypeStruct((tok, width), jnp.bfloat16),
        in_specs=[hbm] * 9,
        out_specs=pl.BlockSpec(memory_space=pltpu.VMEM),
        scratch_shapes=[
            pltpu.VMEM((1, text_count.shape[0]), jnp.int32),
            pltpu.VMEM(hidden.shape, hidden.dtype),
            pltpu.VMEM(query_gain.shape, query_gain.dtype),
            pltpu.VMEM(key_gain.shape, key_gain.dtype),
            pltpu.VMEM(gate_table.shape, gate_table.dtype),
            pltpu.VMEM((3, tok, width), jnp.bfloat16),
            pltpu.VMEM((3, chips, 2) + block, jnp.bfloat16),
            pltpu.VMEM((own_heads, 3, chips, 2) + block, jnp.bfloat16),
            pltpu.VMEM((own_heads, tokens, tokens), jnp.bfloat16),
            pltpu.VMEM((chips,) + block, jnp.bfloat16),
            pltpu.VMEM((own_heads, chips, 2) + block, jnp.bfloat16),
            pltpu.VMEM((heads,) + block, jnp.bfloat16),
            pltpu.VMEM((chips, 2, 1, tok), jnp.int32),
            pltpu.VMEM((devices, tok, LANES), jnp.bfloat16),
            pltpu.VMEM((tokens, tokens), jnp.bfloat16),
            pltpu.VMEM((chips, 2, tok, LANES), jnp.float32),
            pltpu.VMEM((chips, 2, tok, LANES), jnp.float32),
            pltpu.VMEM((chips, 2, tok, tokens), jnp.float32),
            pltpu.VMEM((heads, tok, LANES), jnp.float32),
            regular((levels,)),
            regular,
            regular((levels,)),
            regular,
            regular,
            dma((5,)),
            dma,
            dma((2,)),
            dma((1 + own_heads,)),
            dma((chips - 1,)),
            dma((chips,)),
            dma((4 + 2 * own_heads,)),
            dma((4 + 2 * own_heads,)),
            dma((3 + own_heads,)),
            dma((3 + own_heads,)),
        ],
        compiler_params=pltpu.CompilerParams(
            collective_id=0, has_side_effects=True, vmem_limit_bytes=16 * 1024 * 1024
        ),
    )(*(
        pltpu.with_memory_space_constraint(array, pltpu.HBM)
        for array in (
            segment.reshape(1, tok), queries, key_rows, values,
            text_count.reshape(1, -1), hidden, query_gain, key_gain, gate_table,
        )
    ))


def program(*arrays):
    devices = lax.axis_size("seq")
    tok, width = arrays[0].shape
    requests = arrays[-1].shape[0]
    whole_heads = devices % 8 == 0 and (width // HEAD_DIM) % (devices // 2) == 0
    odd = whole_heads and width // HEAD_DIM // (devices // 2) % 2 == 1
    if odd and devices * tok <= 512 and requests <= LANES and tok % 16 == 0:
        return fused(*arrays)
    return per_device(*arrays)


def solution(mesh):
    return jax.shard_map(
        program,
        mesh=mesh,
        in_specs=(
            P(("groups", "seq"), None),
            P(("groups", "seq"), None),
            P(("groups", "seq"), None),
            P(("groups", "seq"), None),
            P(),
            P(),
            P("groups", None, None),
            P(("groups", "seq")),
            P("groups"),
        ),
        out_specs=P(("groups", "seq"), None),
        check_vma=False,
    )
```

time: 30.8 us -> 27.5 us (0.89)
  Pallas kernels: 29 us -> 26.7 us
  local copies, waits for them, and re-layouts: 1.62 us -> 0.68 us
    pallas_call x1, Pallas kernels: 29 us -> 26.7 us  [fused(): pl.pallas_call(functools.partial(fused_kernel, devices), out_shape=jax.Sh...]
    unnamed x1, local copies, waits for them, and re-layouts: 1.62 us -> 0.68 us
where the time goes in v1:
time: 27.5 us; the launch traced here: 27.4 us
  Pallas kernels  26.7 us (97%)
  local copies, waits for them, and re-layouts  0.68 us (2%)
    pallas_call x1, Pallas kernels, fused(): pl.pallas_call(functools.partial(fused_kernel, devices), out_shape=jax.Sh...  26.7 us
    unnamed x1, local copies, waits for them, and re-layouts  0.68 us

profile of v1, /device:TPU:0, one launch (start us, length us, event | category | flops | bytes accessed | tf_op | source)
XLA Modules:
  0.0 27.4 jit_solution(753035466876535248)
XLA Ops:
  0.0 26.7 %shard_map.91 = bf16[32,3072]{1,0:T(8,128)(2,1)S(1)} custom-call(s32[1,32]{1,0:T(1,128)} %bitcast.2, bf16[32,3072]{1,0:T(8,128)(2,1)} %query_hbm.1, bf16[32,3072]{1,0:T(8,128)(2,1)} %key_hbm.1, bf16[32,3072]{1,0:T(8,128)(2,1)} %value_hbm.1, s32[1,4]{1,0:T(1,128)} %bitcast.3, bf16[32,3072]{1,0:T(8,128)(2,1)} %hidden_hbm.1, f32[2,128]{1,0:T(2,128)} %query_gain_hbm.1, ...), custom_call_target="tpu_custom_call" | custom-call | tf_op jit(solution)/shard_map/pallas_call | solution.py:491
  26.7 0.7 %copy.11 = bf16[32,3072]{1,0:T(8,128)(2,1)} copy(bf16[32,3072]{1,0:T(8,128)(2,1)S(1)} %shard_map.91) | data formatting | bytes 393216

commit v2 on v1

--- a/solution.py
+++ b/solution.py
@@ -123,6 +123,7 @@
 
 LANES = 128
 CONTRACT_LAST = (((1,), (1,)), ((), ()))
+FIRST_CORE = (1, 0)
 
 
 def normed(rows, gain_rows):
@@ -137,8 +138,7 @@
     text_ref, hidden_ref, query_gain_ref, key_gain_ref, gate_ref,
     staged, shared, owned, weights, shared_out, owned_out, back, seg_all, hot, earlier,
     query_gains, key_gains, bias, gate_rows,
-    level_sem, row_sem, across_sem, core_sem, pair_sem,
-    load_sem, seg_own_sem, stage_sem, slot_sem,
+    here_sem, go_sem, load_sem, seg_own_sem, stage_sem, slot_sem,
     seg_send, seg_recv, send_sem, recv_sem, relay_send, relay_recv,
 ):
     chips = devices // 2
@@ -179,25 +179,72 @@
     toward = 1 - 2 * (level // (levels // 2))
     near_first = [(level + levels + toward * step) % levels for step in range(1, levels)]
     far_first = [(level + levels - toward * step) % levels for step in range(1, levels)]
+    orders = []
+    for start in range(levels):
+        first = start + (1 if start < levels // 2 else -1)
+        rest = list(range(start - 1, -1, -1)) + list(range(start + 1, levels))
+        orders.append([first] + [n for n in rest if n != first])
+
+    def pick(values):
+        result = values[0]
+        for start in range(1, levels):
+            result = jnp.where(level == start, values[start], result)
+        return result
+
+    met = [pick([order[place] for order in orders]) for place in range(levels - 1)]
+    near_chips = []
+    for place, a_level in enumerate(near_first):
+        near_chips.append(chip_at(a_level, row))
+        near_chips.append(chip_at(a_level, 1 - row))
+    near_chips.append(chip_at(level, 1 - row))
+    far_chips = []
+    for a_level in far_first:
+        far_chips += [chip_at(a_level, 1 - row), chip_at(a_level, row)]
+    far_chips.append(chip_at(level, 1 - row))
+
+    for part in range(2):
+        pltpu.make_async_copy(sources[part], staged.at[part], stage_sem.at[0]).start()
 
     barrier = pltpu.get_barrier_semaphore()
-    for step in range(1, levels):
-        @pl.when(level + step < levels)
+
+    @pl.when(me > 0)
+    def _():
+        pl.semaphore_wait(barrier, (level + levels - 1) // levels + row + core)
+
+    @pl.when(level + 1 < levels)
+    def _():
+        signal(barrier, me + 4)
+
+    @pl.when(row == 0)
+    def _():
+        signal(barrier, me + 2)
+
+    @pl.when(core == 0)
+    def _():
+        signal(barrier, me + 1)
+
+    for down in range(levels):
+        for row_down in range(2):
+            for core_down in range(2):
+                if down + row_down + core_down > 0:
+                    fits = level >= down
+                    if row_down:
+                        fits = jnp.logical_and(fits, row == 1)
+                    if core_down:
+                        fits = jnp.logical_and(fits, core == 1)
+
+                    @pl.when(fits)
+                    def _():
+                        signal(here_sem.at[me], me - 4 * down - 2 * row_down - core_down)
+
+    def vouched(condition, a_level, a_row, a_core):
+        @pl.when(condition)
         def _():
-            signal(barrier, chip_at(level + step, row) * 2 + core)
-
-    @pl.when(row == 0)
-    def _():
-        signal(barrier, chip_at(level, 1) * 2 + core)
-
-    @pl.when(core == 0)
-    def _():
-        signal(barrier, partner)
+            pl.semaphore_wait(here_sem.at[chip_at(a_level, a_row) * 2 + a_core], 1)
 
     seg_own = pltpu.make_async_copy(segment_hbm, seg_all.at[chip, core], seg_own_sem)
     seg_own.start()
-    for part, source in enumerate(sources):
-        pltpu.make_async_copy(source, staged.at[part], stage_sem.at[part // 2]).start()
+    pltpu.make_async_copy(sources[2], staged.at[2], stage_sem.at[1]).start()
     for part, source in enumerate(sources):
         pltpu.make_async_copy(
             source.at[:, columns(chip * per_chip)], shared.at[part, chip, core], slot_sem.at[0]
@@ -218,112 +265,119 @@
     ]
     for copy in loads:
         copy.start()
+    settle(staged.at[0:2], stage_sem.at[0])
     seg_own.wait()
-    settle(staged.at[0:2], stage_sem.at[0])
-
-    @pl.when(me > 0)
-    def _():
-        pl.semaphore_wait(barrier, level + row + core)
-
-    for step in range(1, levels):
-        @pl.when(level >= step)
-        def _():
-            signal(level_sem.at[level], chip_at(level - step, row) * 2 + core)
-
-    @pl.when(row == 1)
-    def _():
-        signal(row_sem, chip_at(level, 0) * 2 + core)
-
-    @pl.when(core == 1)
-    def _():
-        signal(core_sem, partner)
 
     seg_copies = []
+
+    def own_head(j, a_core):
+        return 1 + a_core * own_heads + j
+
+    def send_owned(parts, place, j, to_chip, a_core):
+        remote(
+            staged.at[parts, :, columns(to_chip * per_chip + own_head(j, a_core))],
+            owned.at[j, parts, chip, core],
+            send_sem.at[place + 2 * j], recv_sem.at[place + 2 * j], to_chip * 2 + a_core,
+        )
 
     def send_shared(to_chip):
         seg_copies.append(remote(
             seg_all.at[chip, core], seg_all.at[chip, core],
             seg_send.at[len(seg_copies)], seg_recv.at[chip], to_chip * 2 + core,
         ))
+        cols = columns(to_chip * per_chip)
         remote(
-            staged.at[0:2, :, columns(to_chip * per_chip)], shared.at[0:2, chip, core],
+            staged.at[0:2, :, cols], shared.at[0:2, chip, core],
             send_sem.at[0], recv_sem.at[0], to_chip * 2 + core,
         )
-
-    def meet(a_level):
-        @pl.when(a_level > level)
-        def _():
-            pl.semaphore_wait(level_sem.at[a_level], 1)
-
-    meet(near_first[0])
-    send_shared(chip_at(near_first[0], row))
-
-    @pl.when(row == 0)
-    def _():
-        pl.semaphore_wait(row_sem, 1)
-
-    signal(across_sem.at[level], chip_at(near_first[0], row) * 2 + core)
-    send_shared(chip_at(level, 1 - row))
-    for a_level in near_first[1:]:
-        meet(a_level)
-        signal(across_sem.at[level], chip_at(a_level, row) * 2 + core)
-        send_shared(chip_at(a_level, row))
-    for a_level in near_first:
-        pl.semaphore_wait(across_sem.at[a_level], 1)
-        send_shared(chip_at(a_level, 1 - row))
-
-    near_chips = [chip_at(a, row) for a in near_first] + [chip_at(level, 1 - row)]
-    near_chips += [chip_at(a, 1 - row) for a in near_first]
-    far_chips = [chip_at(a, 1 - row) for a in far_first] + [chip_at(a, row) for a in far_first]
-    far_chips += [chip_at(level, 1 - row)]
-
-    settle(staged.at[2], stage_sem.at[1])
-    for to_chip in near_chips:
         remote(
-            staged.at[2, :, columns(to_chip * per_chip)], shared.at[2, chip, core],
+            staged.at[2, :, cols], shared.at[2, chip, core],
             send_sem.at[1], recv_sem.at[1], to_chip * 2 + core,
         )
 
-    @pl.when(core == 0)
-    def _():
-        pl.semaphore_wait(core_sem, 1)
-
-    for to_chip in near_chips:
-        signal(pair_sem, to_chip * 2 + core)
-
-    def own_head(j, a_core):
-        return 1 + a_core * own_heads + j
-
-    beside = [
-        remote(
+    settle(staged.at[2], stage_sem.at[1])
+    low = core == 0
+    upper = row == 0
+    low_upper = jnp.logical_and(low, upper)
+
+    def send_query_key(to_chip, a_core):
+        for j in range(own_heads):
+            send_owned(slice(0, 2), 5, j, to_chip, a_core)
+
+    def send_value(to_chip, a_core):
+        for j in range(own_heads):
+            send_owned(2, 6, j, to_chip, a_core)
+
+    def send_all_owned(to_chips):
+        for to_chip in to_chips:
+            send_query_key(to_chip, FIRST_CORE[0])
+            send_value(to_chip, FIRST_CORE[0])
+        for to_chip in to_chips:
+            send_query_key(to_chip, FIRST_CORE[1])
+        for to_chip in to_chips:
+            send_value(to_chip, FIRST_CORE[1])
+
+    beside = []
+    for place, a_level in enumerate(met):
+        above = a_level > level
+        vouched(above, a_level, row, core)
+        send_shared(chip_at(a_level, row))
+        if place == 0:
+            vouched(low, level, row, 1)
+            vouched(jnp.logical_and(low, above), a_level, row, 1)
+            send_all_owned([chip_at(a_level, row)])
+            continue
+        if place == 1:
+            vouched(upper, level, 1, core)
+            send_shared(chip_at(level, 1 - row))
+            vouched(jnp.logical_and(met[0] > level, upper), met[0], 1, core)
+            send_shared(chip_at(met[0], 1 - row))
+        vouched(jnp.logical_and(above, upper), a_level, 1, core)
+        send_shared(chip_at(a_level, 1 - row))
+
+    for j in range(own_heads):
+        beside.append(remote(
             staged.at[:, :, columns(chip * per_chip + own_head(j, 1 - core))],
             owned.at[j, :, chip, core], relay_send.at[3 + j], relay_recv.at[3 + j], partner,
-        )
-        for j in range(own_heads)
-    ]
+        ))
+    vouched(low_upper, level, 1, 1)
+    vouched(jnp.logical_and(low_upper, met[0] > level), met[0], 1, 1)
+    for a_level in met[1:]:
+        vouched(jnp.logical_and(low, a_level > level), a_level, row, 1)
+        vouched(jnp.logical_and(low_upper, a_level > level), a_level, 1, 1)
+
+    across_chips = []
+    for a_level in met[1:]:
+        across_chips += [chip_at(a_level, row), chip_at(a_level, 1 - row)]
+    beside_chips = [chip_at(met[0], 1 - row), chip_at(level, 1 - row)]
+    inner = jnp.logical_or(level == levels // 2 - 1, level == levels // 2)
+
+    @pl.when(inner)
+    def _():
+        send_all_owned(beside_chips[0:1] + across_chips + beside_chips[1:])
+
+    @pl.when(jnp.logical_not(inner))
+    def _():
+        send_all_owned(beside_chips)
 
     earlier[...] = (
         lax.broadcasted_iota(jnp.int32, (tokens, tokens), 1)
         < lax.broadcasted_iota(jnp.int32, (tokens, tokens), 0)
     ).astype(jnp.float32).astype(jnp.bfloat16)
 
-    pl.semaphore_wait(pair_sem, chips - 1)
-    for j in range(own_heads):
-        for to_chip in near_chips:
-            for a_core in range(2):
-                remote(
-                    staged.at[0:2, :, columns(to_chip * per_chip + own_head(j, a_core))],
-                    owned.at[j, 0:2, chip, core],
-                    send_sem.at[4 + 2 * j], recv_sem.at[4 + 2 * j], to_chip * 2 + a_core,
-                )
-    for j in range(own_heads):
-        for to_chip in far_chips:
-            for a_core in range(2):
-                remote(
-                    staged.at[2, :, columns(to_chip * per_chip + own_head(j, a_core))],
-                    owned.at[j, 2, chip, core],
-                    send_sem.at[5 + 2 * j], recv_sem.at[5 + 2 * j], to_chip * 2 + a_core,
-                )
+    shared_sends = (shared.at[0:2, 0 : chips - 1, 0], shared.at[2, 0 : chips - 1, 0])
+
+    @pl.when(inner)
+    def _():
+        for place in range(2):
+            settle(shared_sends[place], send_sem.at[place])
+        for step in range(1, levels // 2):
+            signal(go_sem, chip_at(level - toward * step, row) * 2 + core)
+
+    @pl.when(jnp.logical_not(inner))
+    def _():
+        pl.semaphore_wait(go_sem, 1)
+        send_all_owned(across_chips)
 
     for step in range(1, chips):
         source = (chip + step) % chips
@@ -392,11 +446,6 @@
     shared_out[...] = jnp.dot(
         part_weights, shared[2].reshape(full), preferred_element_type=jnp.float32
     ).astype(jnp.bfloat16).reshape(chips, tok, HEAD_DIM)
-    for to_chip in far_chips:
-        remote(
-            shared_out.at[to_chip], back.at[chip * per_chip],
-            send_sem.at[2], recv_sem.at[2], to_chip * 2 + core,
-        )
 
     number = lax.broadcasted_iota(jnp.int32, (LANES, LANES), 0).astype(jnp.float32)
     own_id = jnp.dot(hot[me], number.astype(jnp.bfloat16), preferred_element_type=jnp.float32)
@@ -423,13 +472,20 @@
 
     for j in range(own_heads):
         settle(owned.at[j, :, chip, core], slot_sem.at[1 + j])
-        settle(owned.at[j, 0:2, 0 : chips - 1], recv_sem.at[4 + 2 * j])
+        settle(owned.at[j, 0:2, 0 : chips - 1], recv_sem.at[5 + 2 * j])
         beside[j].wait_recv()
+        if j == 0:
+            for to_chip in far_chips:
+                remote(
+                    shared_out.at[to_chip], back.at[chip * per_chip],
+                    send_sem.at[2], recv_sem.at[2], to_chip * 2 + core,
+                )
         query_n = normed(owned[j, 0], query_gains[...]).reshape(full)
         key_n = normed(owned[j, 1], key_gains[...]).reshape(full)
         weights[j] = attention_weights(query_n, key_n, bias[...].reshape(tokens, tokens))
+    across = []
     for j in range(own_heads):
-        settle(owned.at[j, 2, 0 : chips - 1], recv_sem.at[5 + 2 * j])
+        settle(owned.at[j, 2, 0 : chips - 1], recv_sem.at[6 + 2 * j])
         owned_out[j] = jnp.dot(
             weights[j], owned[j, 2].reshape(full), preferred_element_type=jnp.float32
         ).astype(jnp.bfloat16).reshape(chips, 2, tok, HEAD_DIM)
@@ -438,12 +494,12 @@
             for a_core in range(2):
                 remote(
                     owned_out.at[j, to_chip, a_core], back.at[head],
-                    send_sem.at[3], recv_sem.at[3], to_chip * 2 + a_core,
+                    send_sem.at[3], recv_sem.at[3 + core], to_chip * 2 + a_core,
                 )
-        remote(
+        across.append(remote(
             owned_out.at[j, chip, 1 - core], back.at[head],
-            send_sem.at[3], recv_sem.at[3], partner,
-        )
+            relay_send.at[3 + own_heads + j], relay_recv.at[3 + own_heads + j], partner,
+        ))
 
     def finish(head):
         cols = slice(head * HEAD_DIM, (head + 1) * HEAD_DIM)
@@ -452,26 +508,35 @@
             + gate_rows[head] * back[head].astype(jnp.float32)
         ).astype(jnp.bfloat16)
 
+    for copy in seg_copies + [seg_relay] + relays + beside:
+        copy.wait_send()
+
+    @pl.when(jnp.logical_not(inner))
+    def _():
+        for place in range(2):
+            settle(shared_sends[place], send_sem.at[place])
+
+    for j in range(own_heads):
+        settle(owned.at[j, 0:2, 0 : chips - 1], send_sem.at[5 + 2 * j])
+        settle(owned.at[j, 2, 0 : chips - 1], send_sem.at[6 + 2 * j])
     back[chip * per_chip] = shared_out[chip]
     settle(back.at[0 : chips - 1], recv_sem.at[2])
     for a_chip in range(chips):
         finish(a_chip * per_chip)
     for j in range(own_heads):
         back[chip * per_chip + own_head(j, core)] = owned_out.at[j, chip, core][...]
-    settle(back.at[0 : own_heads * (devices - 1)], recv_sem.at[3])
-    for a_chip in range(chips):
-        for head in range(1, per_chip):
-            finish(a_chip * per_chip + head)
-
-    for copy in seg_copies + [seg_relay] + relays + beside:
+    for copy in across:
+        copy.wait_recv()
+    for a_core in FIRST_CORE:
+        settle(back.at[0 : own_heads * (chips - 1)], recv_sem.at[3 + a_core])
+        for a_chip in range(chips):
+            for j in range(own_heads):
+                finish(a_chip * per_chip + own_head(j, a_core))
+
+    for copy in across:
         copy.wait_send()
-    settle(shared.at[0:2, 0 : chips - 1, 0], send_sem.at[0])
-    settle(shared.at[2, 0 : chips - 1, 0], send_sem.at[1])
     settle(back.at[0 : chips - 1], send_sem.at[2])
-    settle(back.at[0 : own_heads * (devices - 1)], send_sem.at[3])
-    for j in range(own_heads):
-        settle(owned.at[j, 0:2, 0 : chips - 1], send_sem.at[4 + 2 * j])
-        settle(owned.at[j, 2, 0 : chips - 1], send_sem.at[5 + 2 * j])
+    settle(back.at[0 : 2 * own_heads * (chips - 1)], send_sem.at[3])
 
 
 def fused(
@@ -479,7 +544,6 @@
 ):
     devices = lax.axis_size("seq")
     chips = devices // 2
-    levels = chips // 2
     tok, width = hidden.shape
     heads = width // HEAD_DIM
     own_heads = heads // chips // 2
@@ -487,7 +551,6 @@
     hbm = pl.BlockSpec(memory_space=pl.ANY)
     block = (tok, HEAD_DIM)
     dma = pltpu.SemaphoreType.DMA
-    regular = pltpu.SemaphoreType.REGULAR
     return pl.pallas_call(
         functools.partial(fused_kernel, devices),
         out_shape=jax.ShapeDtypeStruct((tok, width), jnp.bfloat16),
@@ -513,21 +576,18 @@
             pltpu.VMEM((chips, 2, tok, LANES), jnp.float32),
             pltpu.VMEM((chips, 2, tok, tokens), jnp.float32),
             pltpu.VMEM((heads, tok, LANES), jnp.float32),
-            regular((levels,)),
-            regular,
-            regular((levels,)),
-            regular,
-            regular,
+            pltpu.SemaphoreType.REGULAR((devices,)),
+            pltpu.SemaphoreType.REGULAR,
             dma((5,)),
             dma,
             dma((2,)),
             dma((1 + own_heads,)),
             dma((chips - 1,)),
             dma((chips,)),
-            dma((4 + 2 * own_heads,)),
-            dma((4 + 2 * own_heads,)),
-            dma((3 + own_heads,)),
-            dma((3 + own_heads,)),
+            dma((5 + 2 * own_heads,)),
+            dma((5 + 2 * own_heads,)),
+            dma((3 + 2 * own_heads,)),
+            dma((3 + 2 * own_heads,)),
         ],
         compiler_params=pltpu.CompilerParams(
             collective_id=0, has_side_effects=True, vmem_limit_bytes=16 * 1024 * 1024

time: 27.5 us -> 26.9 us (0.978)
  Pallas kernels: 26.7 us -> 26 us
    pallas_call x1, Pallas kernels: 26.7 us -> 26 us  [fused(): pl.pallas_call(functools.partial(fused_kernel, devices), out_shape=jax.Sh...]
where the time goes in v2:
time: 26.9 us; the launch traced here: 26.7 us
  Pallas kernels  26 us (97%)
  local copies, waits for them, and re-layouts  0.68 us (3%)
    pallas_call x1, Pallas kernels, fused(): pl.pallas_call(functools.partial(fused_kernel, devices), out_shape=jax.Sh...  26 us
    unnamed x1, local copies, waits for them, and re-layouts  0.68 us

profile of v2, /device:TPU:0, one launch (start us, length us, event | category | flops | bytes accessed | tf_op | source)
XLA Modules:
  0.0 26.7 jit_solution(11106716561481407762)
XLA Ops:
  0.0 26.0 %shard_map.91 = bf16[32,3072]{1,0:T(8,128)(2,1)S(1)} custom-call(s32[1,32]{1,0:T(1,128)} %bitcast.2, bf16[32,3072]{1,0:T(8,128)(2,1)} %query_hbm.1, bf16[32,3072]{1,0:T(8,128)(2,1)} %key_hbm.1, bf16[32,3072]{1,0:T(8,128)(2,1)} %value_hbm.1, s32[1,4]{1,0:T(1,128)} %bitcast.3, bf16[32,3072]{1,0:T(8,128)(2,1)} %hidden_hbm.1, f32[2,128]{1,0:T(2,128)} %query_gain_hbm.1, ...), custom_call_target="tpu_custom_call" | custom-call | tf_op jit(solution)/shard_map/pallas_call | solution.py:554
  26.1 0.7 %copy.11 = bf16[32,3072]{1,0:T(8,128)(2,1)} copy(bf16[32,3072]{1,0:T(8,128)(2,1)S(1)} %shard_map.91) | data formatting | bytes 393216

commit v3 on v2

--- a/solution.py
+++ b/solution.py
@@ -123,7 +123,6 @@
 
 LANES = 128
 CONTRACT_LAST = (((1,), (1,)), ((), ()))
-FIRST_CORE = (1, 0)
 
 
 def normed(rows, gain_rows):
@@ -136,10 +135,10 @@
     devices, segment_hbm, query_hbm, key_hbm, value_hbm,
     text_hbm, hidden_hbm, query_gain_hbm, key_gain_hbm, gate_hbm, out_ref,
     text_ref, hidden_ref, query_gain_ref, key_gain_ref, gate_ref,
-    staged, shared, owned, weights, shared_out, owned_out, back, seg_all, hot, earlier,
+    staged, shared, owned, shared_out, owned_out, back, seg_all, hot, earlier,
     query_gains, key_gains, bias, gate_rows,
     here_sem, go_sem, load_sem, seg_own_sem, stage_sem, slot_sem,
-    seg_send, seg_recv, send_sem, recv_sem, relay_send, relay_recv,
+    seg_recv, send_sem, recv_sem, relay_recv,
 ):
     chips = devices // 2
     levels = chips // 2
@@ -199,11 +198,11 @@
     near_chips.append(chip_at(level, 1 - row))
     far_chips = []
     for a_level in far_first:
-        far_chips += [chip_at(a_level, 1 - row), chip_at(a_level, row)]
+        far_chips += [chip_at(a_level, 0), chip_at(a_level, 1)]
     far_chips.append(chip_at(level, 1 - row))
 
-    for part in range(2):
-        pltpu.make_async_copy(sources[part], staged.at[part], stage_sem.at[0]).start()
+    for part, source in enumerate(sources):
+        pltpu.make_async_copy(source, staged.at[part], stage_sem).start()
 
     barrier = pltpu.get_barrier_semaphore()
 
@@ -244,15 +243,14 @@
 
     seg_own = pltpu.make_async_copy(segment_hbm, seg_all.at[chip, core], seg_own_sem)
     seg_own.start()
-    pltpu.make_async_copy(sources[2], staged.at[2], stage_sem.at[1]).start()
     for part, source in enumerate(sources):
         pltpu.make_async_copy(
-            source.at[:, columns(chip * per_chip)], shared.at[part, chip, core], slot_sem.at[0]
+            source.at[:, columns(chip * per_chip)], shared.at[part, chip, core], slot_sem
         ).start()
         for j in range(own_heads):
             pltpu.make_async_copy(
                 source.at[:, columns(chip * per_chip + 1 + core * own_heads + j)],
-                owned.at[j, part, chip, core], slot_sem.at[1 + j],
+                owned.at[j, part, me], slot_sem,
             ).start()
     loads = [
         pltpu.make_async_copy(source, target, load_sem.at[place])
@@ -265,67 +263,48 @@
     ]
     for copy in loads:
         copy.start()
-    settle(staged.at[0:2], stage_sem.at[0])
+    settle(staged, stage_sem)
     seg_own.wait()
-
-    seg_copies = []
 
     def own_head(j, a_core):
         return 1 + a_core * own_heads + j
 
-    def send_owned(parts, place, j, to_chip, a_core):
+    def send_owned(to_chip, a_core):
+        for j in range(own_heads):
+            remote(
+                staged.at[:, :, columns(to_chip * per_chip + own_head(j, a_core))],
+                owned.at[j, :, me], send_sem.at[1], recv_sem.at[2 + j], to_chip * 2 + a_core,
+            )
+
+    def send_shared(to_chip):
+        device = to_chip * 2 + core
+        own_ids = seg_all.at[chip, core]
+        remote(own_ids, own_ids, send_sem.at[0], seg_recv, device)
         remote(
-            staged.at[parts, :, columns(to_chip * per_chip + own_head(j, a_core))],
-            owned.at[j, parts, chip, core],
-            send_sem.at[place + 2 * j], recv_sem.at[place + 2 * j], to_chip * 2 + a_core,
+            staged.at[:, :, columns(to_chip * per_chip)], shared.at[:, chip, core],
+            send_sem.at[0], recv_sem.at[0], device,
         )
 
-    def send_shared(to_chip):
-        seg_copies.append(remote(
-            seg_all.at[chip, core], seg_all.at[chip, core],
-            seg_send.at[len(seg_copies)], seg_recv.at[chip], to_chip * 2 + core,
-        ))
-        cols = columns(to_chip * per_chip)
-        remote(
-            staged.at[0:2, :, cols], shared.at[0:2, chip, core],
-            send_sem.at[0], recv_sem.at[0], to_chip * 2 + core,
-        )
-        remote(
-            staged.at[2, :, cols], shared.at[2, chip, core],
-            send_sem.at[1], recv_sem.at[1], to_chip * 2 + core,
-        )
-
-    settle(staged.at[2], stage_sem.at[1])
     low = core == 0
     upper = row == 0
     low_upper = jnp.logical_and(low, upper)
 
-    def send_query_key(to_chip, a_core):
-        for j in range(own_heads):
-            send_owned(slice(0, 2), 5, j, to_chip, a_core)
-
-    def send_value(to_chip, a_core):
-        for j in range(own_heads):
-            send_owned(2, 6, j, to_chip, a_core)
-
-    def send_all_owned(to_chips):
-        for to_chip in to_chips:
-            send_query_key(to_chip, FIRST_CORE[0])
-            send_value(to_chip, FIRST_CORE[0])
-        for to_chip in to_chips:
-            send_query_key(to_chip, FIRST_CORE[1])
-        for to_chip in to_chips:
-            send_value(to_chip, FIRST_CORE[1])
-
-    beside = []
     for place, a_level in enumerate(met):
         above = a_level > level
         vouched(above, a_level, row, core)
         send_shared(chip_at(a_level, row))
         if place == 0:
+            @pl.when(low)
+            def _():
+                send_owned(chip_at(met[0], row), 0)
+
             vouched(low, level, row, 1)
             vouched(jnp.logical_and(low, above), a_level, row, 1)
-            send_all_owned([chip_at(a_level, row)])
+
+            @pl.when(jnp.logical_not(low))
+            def _():
+                send_owned(chip_at(met[0], row), 0)
+
             continue
         if place == 1:
             vouched(upper, level, 1, core)
@@ -335,59 +314,75 @@
         vouched(jnp.logical_and(above, upper), a_level, 1, core)
         send_shared(chip_at(a_level, 1 - row))
 
-    for j in range(own_heads):
-        beside.append(remote(
-            staged.at[:, :, columns(chip * per_chip + own_head(j, 1 - core))],
-            owned.at[j, :, chip, core], relay_send.at[3 + j], relay_recv.at[3 + j], partner,
-        ))
+    send_owned(chip, 1 - core)
     vouched(low_upper, level, 1, 1)
     vouched(jnp.logical_and(low_upper, met[0] > level), met[0], 1, 1)
     for a_level in met[1:]:
         vouched(jnp.logical_and(low, a_level > level), a_level, row, 1)
         vouched(jnp.logical_and(low_upper, a_level > level), a_level, 1, 1)
 
-    across_chips = []
-    for a_level in met[1:]:
-        across_chips += [chip_at(a_level, row), chip_at(a_level, 1 - row)]
-    beside_chips = [chip_at(met[0], 1 - row), chip_at(level, 1 - row)]
+    far_pairs = [(chip_at(a_level, 1 - row), chip_at(a_level, row)) for a_level in far_first]
+    next_door = chip_at(level, 1 - row)
+    across_chips = [to_chip for pair in far_pairs[:-1] for to_chip in pair]
+
+    def send_all_owned(to_chips, last_chips):
+        for to_chip in to_chips:
+            send_owned(to_chip, 0)
+        for to_chip in to_chips + last_chips:
+            send_owned(to_chip, 1)
+
     inner = jnp.logical_or(level == levels // 2 - 1, level == levels // 2)
 
     @pl.when(inner)
     def _():
-        send_all_owned(beside_chips[0:1] + across_chips + beside_chips[1:])
-
-    @pl.when(jnp.logical_not(inner))
-    def _():
-        send_all_owned(beside_chips)
+        send_all_owned(across_chips + [far_pairs[-1][0], next_door], [far_pairs[-1][1]])
 
     earlier[...] = (
         lax.broadcasted_iota(jnp.int32, (tokens, tokens), 1)
         < lax.broadcasted_iota(jnp.int32, (tokens, tokens), 0)
     ).astype(jnp.float32).astype(jnp.bfloat16)
 
-    shared_sends = (shared.at[0:2, 0 : chips - 1, 0], shared.at[2, 0 : chips - 1, 0])
-
-    @pl.when(inner)
-    def _():
-        for place in range(2):
-            settle(shared_sends[place], send_sem.at[place])
+    def settle_shared_sends():
+        settle(shared.at[:, 0 : chips - 1, 0], send_sem.at[0])
+        settle(seg_all.at[0 : chips - 1, 0], send_sem.at[0])
+
+    lower = level < levels // 2
+    outer = jnp.logical_not(inner)
+    lower_outer = jnp.logical_and(lower, outer)
+
+    @pl.when(outer)
+    def _():
+        send_all_owned([far_pairs[-1][0], next_door], [far_pairs[-1][1]])
+
+    @pl.when(jnp.logical_not(lower_outer))
+    def _():
+        settle_shared_sends()
+
+    @pl.when(jnp.logical_and(lower, inner))
+    def _():
         for step in range(1, levels // 2):
-            signal(go_sem, chip_at(level - toward * step, row) * 2 + core)
-
-    @pl.when(jnp.logical_not(inner))
+            signal(go_sem, chip_at(level - step, row) * 2 + core)
+
+    @pl.when(lower_outer)
     def _():
         pl.semaphore_wait(go_sem, 1)
-        send_all_owned(across_chips)
-
-    for step in range(1, chips):
-        source = (chip + step) % chips
-        settle(seg_all.at[source, core], seg_recv.at[source])
-    seg_relay = remote(
-        seg_all.at[:, core], seg_all.at[:, core], relay_send.at[0], relay_recv.at[0], partner
-    )
+
+    @pl.when(outer)
+    def _():
+        send_all_owned(across_chips, [])
+
+    settle(seg_all.at[0 : chips - 1, 0], seg_recv)
+    relays = [remote(
+        seg_all.at[:, core], seg_all.at[:, core], send_sem.at[1], relay_recv.at[0], partner
+    )]
+    settle(owned.at[0, :, 0 : 1 + own_heads], slot_sem)
+    settle(shared.at[:, 0 : chips - 1, 0], recv_sem.at[0])
+    relays.append(remote(
+        shared.at[1:3, :, core], shared.at[1:3, :, core], send_sem.at[1], relay_recv.at[1], partner
+    ))
     for copy in loads:
         copy.wait()
-    seg_relay.wait_recv()
+    relays[0].wait_recv()
     eye = (
         lax.broadcasted_iota(jnp.int32, (tok, tok), 0)
         == lax.broadcasted_iota(jnp.int32, (tok, tok), 1)
@@ -425,24 +420,14 @@
         grown = jnp.exp(scores - jnp.max(scores, axis=-1, keepdims=True))
         return (grown * (1.0 / jnp.sum(grown, axis=-1, keepdims=True))).astype(jnp.bfloat16)
 
-    settle(shared.at[:, chip, core], slot_sem.at[0])
-    settle(shared.at[0:2, 0 : chips - 1, 0], recv_sem.at[0])
-    relays = [remote(
-        shared.at[1, :, core], shared.at[1, :, core], relay_send.at[1], relay_recv.at[1], partner
-    )]
-    settle(shared.at[2, 0 : chips - 1, 0], recv_sem.at[1])
-    relays.append(remote(
-        shared.at[2, :, core], shared.at[2, :, core], relay_send.at[2], relay_recv.at[2], partner
-    ))
     half = (tokens // 2, HEAD_DIM)
     full = (tokens, HEAD_DIM)
     query_n = normed(shared.at[0, :, core][...], query_gains.at[:, core][...]).reshape(half)
-    relays[0].wait_recv()
+    relays[1].wait_recv()
     key_n = normed(shared[1], key_gains[...]).reshape(full)
     part_weights = attention_weights(
         query_n, key_n, bias.at[:, core][...].reshape(tokens // 2, tokens)
     )
-    relays[1].wait_recv()
     shared_out[...] = jnp.dot(
         part_weights, shared[2].reshape(full), preferred_element_type=jnp.float32
     ).astype(jnp.bfloat16).reshape(chips, tok, HEAD_DIM)
@@ -470,36 +455,40 @@
                 total = jnp.where(own_code == float(2 * r + s), pair[s : s + 1], total)
         gate_rows[tile] = total
 
+    far_half = 1 - level // (levels // 2)
     for j in range(own_heads):
-        settle(owned.at[j, :, chip, core], slot_sem.at[1 + j])
-        settle(owned.at[j, 0:2, 0 : chips - 1], recv_sem.at[5 + 2 * j])
-        beside[j].wait_recv()
+        settle(owned.at[j, :, 0 : devices - 1], recv_sem.at[2 + j])
         if j == 0:
             for to_chip in far_chips:
                 remote(
                     shared_out.at[to_chip], back.at[chip * per_chip],
-                    send_sem.at[2], recv_sem.at[2], to_chip * 2 + core,
+                    send_sem.at[1], recv_sem.at[1], to_chip * 2 + core,
                 )
-        query_n = normed(owned[j, 0], query_gains[...]).reshape(full)
-        key_n = normed(owned[j, 1], key_gains[...]).reshape(full)
-        weights[j] = attention_weights(query_n, key_n, bias[...].reshape(tokens, tokens))
-    across = []
-    for j in range(own_heads):
-        settle(owned.at[j, 2, 0 : chips - 1], recv_sem.at[6 + 2 * j])
-        owned_out[j] = jnp.dot(
-            weights[j], owned[j, 2].reshape(full), preferred_element_type=jnp.float32
-        ).astype(jnp.bfloat16).reshape(chips, 2, tok, HEAD_DIM)
+        flat = (devices, tok, LANES)
+        key_n = normed(owned[j, 1], key_gains[...].reshape(flat)).reshape(full)
+        value_all = owned[j, 2].reshape(full)
         head = chip * per_chip + own_head(j, core)
-        for to_chip in far_chips:
-            for a_core in range(2):
-                remote(
-                    owned_out.at[j, to_chip, a_core], back.at[head],
-                    send_sem.at[3], recv_sem.at[3 + core], to_chip * 2 + a_core,
-                )
-        across.append(remote(
+        for part in (far_half, 1 - far_half):
+            chip_rows = pl.ds(part * (chips // 2), chips // 2)
+            rows_in = owned.at[j, 0, pl.ds(part * chips, chips)][...]
+            gain_rows = query_gains.at[chip_rows][...].reshape(chips, tok, LANES)
+            bias_rows = bias.at[chip_rows][...].reshape(tokens // 2, tokens)
+            part_weights = attention_weights(normed(rows_in, gain_rows).reshape(half), key_n, bias_rows)
+            owned_out[j, chip_rows] = jnp.dot(
+                part_weights, value_all, preferred_element_type=jnp.float32
+            ).astype(jnp.bfloat16).reshape(chips // 2, 2, tok, HEAD_DIM)
+            for to_chip in far_chips:
+                @pl.when(jnp.logical_and(to_chip // (chips // 2) == part, to_chip != chip))
+                def _():
+                    for a_core in range(2):
+                        remote(
+                            owned_out.at[j, to_chip, a_core], back.at[head],
+                            send_sem.at[1], recv_sem.at[1], to_chip * 2 + a_core,
+                        )
+        remote(
             owned_out.at[j, chip, 1 - core], back.at[head],
-            relay_send.at[3 + own_heads + j], relay_recv.at[3 + own_heads + j], partner,
-        ))
+            send_sem.at[1], recv_sem.at[1], partner,
+        )
 
     def finish(head):
         cols = slice(head * HEAD_DIM, (head + 1) * HEAD_DIM)
@@ -508,35 +497,22 @@
             + gate_rows[head] * back[head].astype(jnp.float32)
         ).astype(jnp.bfloat16)
 
-    for copy in seg_copies + [seg_relay] + relays + beside:
-        copy.wait_send()
-
-    @pl.when(jnp.logical_not(inner))
-    def _():
-        for place in range(2):
-            settle(shared_sends[place], send_sem.at[place])
-
+    @pl.when(lower_outer)
+    def _():
+        settle_shared_sends()
+
+    settle(seg_all.at[:, core], send_sem.at[1])
+    settle(shared.at[1:3, :, core], send_sem.at[1])
     for j in range(own_heads):
-        settle(owned.at[j, 0:2, 0 : chips - 1], send_sem.at[5 + 2 * j])
-        settle(owned.at[j, 2, 0 : chips - 1], send_sem.at[6 + 2 * j])
+        settle(owned.at[j, :, 0 : devices - 1], send_sem.at[1])
+    results = back.at[0 : per_chip * (chips - 1) + own_heads]
+    settle(results, send_sem.at[1])
     back[chip * per_chip] = shared_out[chip]
-    settle(back.at[0 : chips - 1], recv_sem.at[2])
-    for a_chip in range(chips):
-        finish(a_chip * per_chip)
     for j in range(own_heads):
         back[chip * per_chip + own_head(j, core)] = owned_out.at[j, chip, core][...]
-    for copy in across:
-        copy.wait_recv()
-    for a_core in FIRST_CORE:
-        settle(back.at[0 : own_heads * (chips - 1)], recv_sem.at[3 + a_core])
-        for a_chip in range(chips):
-            for j in range(own_heads):
-                finish(a_chip * per_chip + own_head(j, a_core))
-
-    for copy in across:
-        copy.wait_send()
-    settle(back.at[0 : chips - 1], send_sem.at[2])
-    settle(back.at[0 : 2 * own_heads * (chips - 1)], send_sem.at[3])
+    settle(results, recv_sem.at[1])
+    for head in range(chips * per_chip):
+        finish(head)
 
 
 def fused(
@@ -564,8 +540,7 @@
             pltpu.VMEM(gate_table.shape, gate_table.dtype),
             pltpu.VMEM((3, tok, width), jnp.bfloat16),
             pltpu.VMEM((3, chips, 2) + block, jnp.bfloat16),
-            pltpu.VMEM((own_heads, 3, chips, 2) + block, jnp.bfloat16),
-            pltpu.VMEM((own_heads, tokens, tokens), jnp.bfloat16),
+            pltpu.VMEM((own_heads, 3, devices) + block, jnp.bfloat16),
             pltpu.VMEM((chips,) + block, jnp.bfloat16),
             pltpu.VMEM((own_heads, chips, 2) + block, jnp.bfloat16),
             pltpu.VMEM((heads,) + block, jnp.bfloat16),
@@ -580,14 +555,12 @@
             pltpu.SemaphoreType.REGULAR,
             dma((5,)),
             dma,
+            dma,
+            dma,
+            dma,
             dma((2,)),
-            dma((1 + own_heads,)),
-            dma((chips - 1,)),
-            dma((chips,)),
-            dma((5 + 2 * own_heads,)),
-            dma((5 + 2 * own_heads,)),
-            dma((3 + 2 * own_heads,)),
-            dma((3 + 2 * own_heads,)),
+            dma((2 + own_heads,)),
+            dma((2,)),
         ],
         compiler_params=pltpu.CompilerParams(
             collective_id=0, has_side_effects=True, vmem_limit_bytes=16 * 1024 * 1024

time: 26.9 us -> 26.1 us (0.970)
  Pallas kernels: 26 us -> 25.3 us
    pallas_call x1, Pallas kernels: 26 us -> 25.3 us  [fused(): pl.pallas_call(functools.partial(fused_kernel, devices), out_shape=jax.Sh...]
where the time goes in v3:
time: 26.1 us; the launch traced here: 26 us
  Pallas kernels  25.3 us (97%)
  local copies, waits for them, and re-layouts  0.68 us (3%)
    pallas_call x1, Pallas kernels, fused(): pl.pallas_call(functools.partial(fused_kernel, devices), out_shape=jax.Sh...  25.3 us
    unnamed x1, local copies, waits for them, and re-layouts  0.68 us

profile of v3, /device:TPU:0, one launch (start us, length us, event | category | flops | bytes accessed | tf_op | source)
XLA Modules:
  0.0 26.0 jit_solution(18387933478067782949)
XLA Ops:
  0.0 25.3 %shard_map.91 = bf16[32,3072]{1,0:T(8,128)(2,1)S(1)} custom-call(s32[1,32]{1,0:T(1,128)} %bitcast.2, bf16[32,3072]{1,0:T(8,128)(2,1)} %query_hbm.1, bf16[32,3072]{1,0:T(8,128)(2,1)} %key_hbm.1, bf16[32,3072]{1,0:T(8,128)(2,1)} %value_hbm.1, s32[1,4]{1,0:T(1,128)} %bitcast.3, bf16[32,3072]{1,0:T(8,128)(2,1)} %hidden_hbm.1, f32[2,128]{1,0:T(2,128)} %query_gain_hbm.1, ...), custom_call_target="tpu_custom_call" | custom-call | tf_op jit(solution)/shard_map/pallas_call | solution.py:530
  25.3 0.7 %copy.11 = bf16[32,3072]{1,0:T(8,128)(2,1)} copy(bf16[32,3072]{1,0:T(8,128)(2,1)S(1)} %shard_map.91) | data formatting | bytes 393216

commit v4 on v3

--- a/solution.py
+++ b/solution.py
@@ -137,7 +137,7 @@
     text_ref, hidden_ref, query_gain_ref, key_gain_ref, gate_ref,
     staged, shared, owned, shared_out, owned_out, back, seg_all, hot, earlier,
     query_gains, key_gains, bias, gate_rows,
-    here_sem, go_sem, load_sem, seg_own_sem, stage_sem, slot_sem,
+    here_sem, go_sem, done_sem, load_sem, seg_own_sem, stage_sem, slot_sem,
     seg_recv, send_sem, recv_sem, relay_recv,
 ):
     chips = devices // 2
@@ -456,14 +456,33 @@
         gate_rows[tile] = total
 
     far_half = 1 - level // (levels // 2)
+    holder = lower_outer
+    hold = jnp.logical_and(holder, low)
+
+    def send_shared_result(to_chip):
+        remote(
+            shared_out.at[to_chip], back.at[chip * per_chip],
+            send_sem.at[1], recv_sem.at[1], to_chip * 2 + core,
+        )
+
+    def send_owned_result(j, to_chip):
+        for a_core in range(2):
+            remote(
+                owned_out.at[j, to_chip, a_core], back.at[chip * per_chip + own_head(j, core)],
+                send_sem.at[1], recv_sem.at[1], to_chip * 2 + a_core,
+            )
+
     for j in range(own_heads):
         settle(owned.at[j, :, 0 : devices - 1], recv_sem.at[2 + j])
         if j == 0:
+            @pl.when(jnp.logical_and(holder, core == 1))
+            def _():
+                signal(done_sem, partner)
+
             for to_chip in far_chips:
-                remote(
-                    shared_out.at[to_chip], back.at[chip * per_chip],
-                    send_sem.at[1], recv_sem.at[1], to_chip * 2 + core,
-                )
+                @pl.when(jnp.logical_not(jnp.logical_and(hold, to_chip // (chips // 2) == far_half)))
+                def _():
+                    send_shared_result(to_chip)
         flat = (devices, tok, LANES)
         key_n = normed(owned[j, 1], key_gains[...].reshape(flat)).reshape(full)
         value_all = owned[j, 2].reshape(full)
@@ -478,17 +497,26 @@
                 part_weights, value_all, preferred_element_type=jnp.float32
             ).astype(jnp.bfloat16).reshape(chips // 2, 2, tok, HEAD_DIM)
             for to_chip in far_chips:
-                @pl.when(jnp.logical_and(to_chip // (chips // 2) == part, to_chip != chip))
+                now = to_chip // (chips // 2) == part
+                now = jnp.logical_and(now, jnp.logical_not(jnp.logical_and(hold, part == far_half)))
+
+                @pl.when(now)
                 def _():
-                    for a_core in range(2):
-                        remote(
-                            owned_out.at[j, to_chip, a_core], back.at[head],
-                            send_sem.at[1], recv_sem.at[1], to_chip * 2 + a_core,
-                        )
+                    send_owned_result(j, to_chip)
         remote(
             owned_out.at[j, chip, 1 - core], back.at[head],
             send_sem.at[1], recv_sem.at[1], partner,
         )
+
+    @pl.when(hold)
+    def _():
+        pl.semaphore_wait(done_sem, 1)
+        for to_chip in far_chips:
+            @pl.when(to_chip // (chips // 2) == far_half)
+            def _():
+                send_shared_result(to_chip)
+                for j in range(own_heads):
+                    send_owned_result(j, to_chip)
 
     def finish(head):
         cols = slice(head * HEAD_DIM, (head + 1) * HEAD_DIM)
@@ -553,6 +581,7 @@
             pltpu.VMEM((heads, tok, LANES), jnp.float32),
             pltpu.SemaphoreType.REGULAR((devices,)),
             pltpu.SemaphoreType.REGULAR,
+            pltpu.SemaphoreType.REGULAR,
             dma((5,)),
             dma,
             dma,
@@ -578,7 +607,7 @@
     devices = lax.axis_size("seq")
     tok, width = arrays[0].shape
     requests = arrays[-1].shape[0]
-    whole_heads = devices % 8 == 0 and (width // HEAD_DIM) % (devices // 2) == 0
+    whole_heads = devices % 8 == 0 and devices > 8 and (width // HEAD_DIM) % (devices // 2) == 0
     odd = whole_heads and width // HEAD_DIM // (devices // 2) % 2 == 1
     if odd and devices * tok <= 512 and requests <= LANES and tok % 16 == 0:
         return fused(*arrays)

time: 26.1 us -> 25.6 us (0.981)
  Pallas kernels: 25.3 us -> 24.8 us
    pallas_call x1, Pallas kernels: 25.3 us -> 24.8 us  [fused(): pl.pallas_call(functools.partial(fused_kernel, devices), out_shape=jax.Sh...]
where the time goes in v4:
time: 25.6 us; the launch traced here: 25.5 us
  Pallas kernels  24.8 us (97%)
  local copies, waits for them, and re-layouts  0.68 us (3%)
    pallas_call x1, Pallas kernels, fused(): pl.pallas_call(functools.partial(fused_kernel, devices), out_shape=jax.Sh...  24.8 us
    unnamed x1, local copies, waits for them, and re-layouts  0.68 us

profile of v4, /device:TPU:0, one launch (start us, length us, event | category | flops | bytes accessed | tf_op | source)
XLA Modules:
  0.0 25.5 jit_solution(14922778848850137251)
XLA Ops:
  0.0 24.8 %shard_map.91 = bf16[32,3072]{1,0:T(8,128)(2,1)S(1)} custom-call(s32[1,32]{1,0:T(1,128)} %bitcast.2, bf16[32,3072]{1,0:T(8,128)(2,1)} %query_hbm.1, bf16[32,3072]{1,0:T(8,128)(2,1)} %key_hbm.1, bf16[32,3072]{1,0:T(8,128)(2,1)} %value_hbm.1, s32[1,4]{1,0:T(1,128)} %bitcast.3, bf16[32,3072]{1,0:T(8,128)(2,1)} %hidden_hbm.1, f32[2,128]{1,0:T(2,128)} %query_gain_hbm.1, ...), custom_call_target="tpu_custom_call" | custom-call | tf_op jit(solution)/shard_map/pallas_call | solution.py:558
  24.8 0.7 %copy.11 = bf16[32,3072]{1,0:T(8,128)(2,1)} copy(bf16[32,3072]{1,0:T(8,128)(2,1)S(1)} %shard_map.91) | data formatting | bytes 393216

commit v5 on v4

--- a/solution.py
+++ b/solution.py
@@ -135,7 +135,7 @@
     devices, segment_hbm, query_hbm, key_hbm, value_hbm,
     text_hbm, hidden_hbm, query_gain_hbm, key_gain_hbm, gate_hbm, out_ref,
     text_ref, hidden_ref, query_gain_ref, key_gain_ref, gate_ref,
-    staged, shared, owned, shared_out, owned_out, back, seg_all, hot, earlier,
+    staged, shared, owned, passing, shared_out, owned_out, back, seg_all, hot, earlier,
     query_gains, key_gains, bias, gate_rows,
     here_sem, go_sem, done_sem, load_sem, seg_own_sem, stage_sem, slot_sem,
     seg_recv, send_sem, recv_sem, relay_recv,
@@ -196,11 +196,6 @@
         near_chips.append(chip_at(a_level, row))
         near_chips.append(chip_at(a_level, 1 - row))
     near_chips.append(chip_at(level, 1 - row))
-    far_chips = []
-    for a_level in far_first:
-        far_chips += [chip_at(a_level, 0), chip_at(a_level, 1)]
-    far_chips.append(chip_at(level, 1 - row))
-
     for part, source in enumerate(sources):
         pltpu.make_async_copy(source, staged.at[part], stage_sem).start()
 
@@ -325,11 +320,16 @@
     next_door = chip_at(level, 1 - row)
     across_chips = [to_chip for pair in far_pairs[:-1] for to_chip in pair]
 
-    def send_all_owned(to_chips, last_chips):
+    def send_all_owned(to_chips, last_chips, but=None):
         for to_chip in to_chips:
             send_owned(to_chip, 0)
         for to_chip in to_chips + last_chips:
-            send_owned(to_chip, 1)
+            if to_chip is but:
+                @pl.when(jnp.logical_not(shifts))
+                def _():
+                    send_owned(to_chip, 1)
+            else:
+                send_owned(to_chip, 1)
 
     inner = jnp.logical_or(level == levels // 2 - 1, level == levels // 2)
 
@@ -347,6 +347,8 @@
         settle(seg_all.at[0 : chips - 1, 0], send_sem.at[0])
 
     lower = level < levels // 2
+    shifts = jnp.logical_and(lower, row == 1)
+    shifted_chip = chip_at(levels // 2, 0)
     outer = jnp.logical_not(inner)
     lower_outer = jnp.logical_and(lower, outer)
 
@@ -363,13 +365,32 @@
         for step in range(1, levels // 2):
             signal(go_sem, chip_at(level - step, row) * 2 + core)
 
+    passes = jnp.logical_and(lower_outer, row == 0)
+
+    @pl.when(jnp.logical_and(lower_outer, row == 1))
+    def _():
+        for j in range(own_heads):
+            remote(
+                staged.at[:, :, columns(shifted_chip * per_chip + own_head(j, 1))],
+                passing.at[j], send_sem.at[1], relay_recv.at[2], me - 2,
+            )
+
     @pl.when(lower_outer)
     def _():
         pl.semaphore_wait(go_sem, 1)
 
     @pl.when(outer)
     def _():
-        send_all_owned(across_chips, [])
+        send_all_owned(across_chips, [], across_chips[2])
+
+    @pl.when(passes)
+    def _():
+        settle(passing, relay_recv.at[2])
+        for j in range(own_heads):
+            remote(
+                passing.at[j], owned.at[j, :, me + 2],
+                send_sem.at[1], recv_sem.at[2 + j], shifted_chip * 2 + 1,
+            )
 
     settle(seg_all.at[0 : chips - 1, 0], seg_recv)
     relays = [remote(
@@ -455,9 +476,11 @@
                 total = jnp.where(own_code == float(2 * r + s), pair[s : s + 1], total)
         gate_rows[tile] = total
 
-    far_half = 1 - level // (levels // 2)
     holder = lower_outer
     hold = jnp.logical_and(holder, low)
+    lower_half = level < levels // 2
+    lower_chips = list(range(chips // 2))
+    upper_chips = list(range(chips // 2, chips))
 
     def send_shared_result(to_chip):
         remote(
@@ -472,6 +495,18 @@
                 send_sem.at[1], recv_sem.at[1], to_chip * 2 + a_core,
             )
 
+    def send_results(to_chips, condition, send):
+        for to_chip in to_chips:
+            @pl.when(jnp.logical_and(condition, chip != to_chip))
+            def _():
+                send(to_chip)
+
+    def send_shared_results(to_chips, condition):
+        send_results(to_chips, condition, send_shared_result)
+
+    def send_owned_results(j, to_chips, condition):
+        send_results(to_chips, condition, functools.partial(send_owned_result, j))
+
     for j in range(own_heads):
         settle(owned.at[j, :, 0 : devices - 1], recv_sem.at[2 + j])
         if j == 0:
@@ -479,30 +514,30 @@
             def _():
                 signal(done_sem, partner)
 
-            for to_chip in far_chips:
-                @pl.when(jnp.logical_not(jnp.logical_and(hold, to_chip // (chips // 2) == far_half)))
-                def _():
-                    send_shared_result(to_chip)
+            send_shared_results(lower_chips[2:], lower_half)
+            send_shared_results(lower_chips[:2], chip >= 0)
+            send_shared_results(upper_chips, jnp.logical_not(hold))
         flat = (devices, tok, LANES)
         key_n = normed(owned[j, 1], key_gains[...].reshape(flat)).reshape(full)
         value_all = owned[j, 2].reshape(full)
         head = chip * per_chip + own_head(j, core)
-        for part in (far_half, 1 - far_half):
-            chip_rows = pl.ds(part * (chips // 2), chips // 2)
-            rows_in = owned.at[j, 0, pl.ds(part * chips, chips)][...]
-            gain_rows = query_gains.at[chip_rows][...].reshape(chips, tok, LANES)
-            bias_rows = bias.at[chip_rows][...].reshape(tokens // 2, tokens)
-            part_weights = attention_weights(normed(rows_in, gain_rows).reshape(half), key_n, bias_rows)
+        for place, to_chips in enumerate((lower_chips, upper_chips)):
+            chip_rows = pl.ds(place * (chips // 2), chips // 2)
+            rows_in = owned[j, 0, place * chips : (place + 1) * chips]
+            gain_rows = query_gains[chip_rows].reshape(chips, tok, LANES)
+            query_n = normed(rows_in, gain_rows).reshape(half)
+            bias_rows = bias[chip_rows].reshape(tokens // 2, tokens)
             owned_out[j, chip_rows] = jnp.dot(
-                part_weights, value_all, preferred_element_type=jnp.float32
+                attention_weights(query_n, key_n, bias_rows), value_all,
+                preferred_element_type=jnp.float32,
             ).astype(jnp.bfloat16).reshape(chips // 2, 2, tok, HEAD_DIM)
-            for to_chip in far_chips:
-                now = to_chip // (chips // 2) == part
-                now = jnp.logical_and(now, jnp.logical_not(jnp.logical_and(hold, part == far_half)))
-
-                @pl.when(now)
-                def _():
-                    send_owned_result(j, to_chip)
+            if place == 0:
+                send_owned_results(j, lower_chips[:2], chip >= 0)
+                send_owned_results(j, lower_chips[2:], lower_half)
+        send_owned_results(j, lower_chips[2:], jnp.logical_not(lower_half))
+        send_owned_results(j, upper_chips, jnp.logical_not(hold))
+        if j == 0:
+            send_shared_results(lower_chips[2:], jnp.logical_not(lower_half))
         remote(
             owned_out.at[j, chip, 1 - core], back.at[head],
             send_sem.at[1], recv_sem.at[1], partner,
@@ -511,12 +546,10 @@
     @pl.when(hold)
     def _():
         pl.semaphore_wait(done_sem, 1)
-        for to_chip in far_chips:
-            @pl.when(to_chip // (chips // 2) == far_half)
-            def _():
-                send_shared_result(to_chip)
-                for j in range(own_heads):
-                    send_owned_result(j, to_chip)
+        for to_chip in upper_chips:
+            send_shared_result(to_chip)
+            for j in range(own_heads):
+                send_owned_result(j, to_chip)
 
     def finish(head):
         cols = slice(head * HEAD_DIM, (head + 1) * HEAD_DIM)
@@ -528,6 +561,10 @@
     @pl.when(lower_outer)
     def _():
         settle_shared_sends()
+
+    @pl.when(passes)
+    def _():
+        settle(passing, send_sem.at[1])
 
     settle(seg_all.at[:, core], send_sem.at[1])
     settle(shared.at[1:3, :, core], send_sem.at[1])
@@ -569,6 +606,7 @@
             pltpu.VMEM((3, tok, width), jnp.bfloat16),
             pltpu.VMEM((3, chips, 2) + block, jnp.bfloat16),
             pltpu.VMEM((own_heads, 3, devices) + block, jnp.bfloat16),
+            pltpu.VMEM((own_heads, 3) + block, jnp.bfloat16),
             pltpu.VMEM((chips,) + block, jnp.bfloat16),
             pltpu.VMEM((own_heads, chips, 2) + block, jnp.bfloat16),
             pltpu.VMEM((heads,) + block, jnp.bfloat16),
@@ -589,7 +627,7 @@
             dma,
             dma((2,)),
             dma((2 + own_heads,)),
-            dma((2,)),
+            dma((3,)),
         ],
         compiler_params=pltpu.CompilerParams(
             collective_id=0, has_side_effects=True, vmem_limit_bytes=16 * 1024 * 1024

time: 25.6 us -> 25.5 us (level)
  no operation moved by 1% of the time
where the time goes in v5:
time: 25.5 us; the launch traced here: 25.4 us
  Pallas kernels  24.7 us (97%)
  local copies, waits for them, and re-layouts  0.68 us (3%)
    pallas_call x1, Pallas kernels, fused(): pl.pallas_call(functools.partial(fused_kernel, devices), out_shape=jax.Sh...  24.7 us
    unnamed x1, local copies, waits for them, and re-layouts  0.68 us

profile of v5, /device:TPU:0, one launch (start us, length us, event | category | flops | bytes accessed | tf_op | source)
XLA Modules:
  0.0 25.4 jit_solution(12315777840857055090)
XLA Ops:
  0.0 24.7 %shard_map.91 = bf16[32,3072]{1,0:T(8,128)(2,1)S(1)} custom-call(s32[1,32]{1,0:T(1,128)} %bitcast.2, bf16[32,3072]{1,0:T(8,128)(2,1)} %query_hbm.1, bf16[32,3072]{1,0:T(8,128)(2,1)} %key_hbm.1, bf16[32,3072]{1,0:T(8,128)(2,1)} %value_hbm.1, s32[1,4]{1,0:T(1,128)} %bitcast.3, bf16[32,3072]{1,0:T(8,128)(2,1)} %hidden_hbm.1, f32[2,128]{1,0:T(2,128)} %query_gain_hbm.1, ...), custom_call_target="tpu_custom_call" | custom-call | tf_op jit(solution)/shard_map/pallas_call | solution.py:595
  24.7 0.7 %copy.11 = bf16[32,3072]{1,0:T(8,128)(2,1)} copy(bf16[32,3072]{1,0:T(8,128)(2,1)S(1)} %shard_map.91) | data formatting | bytes 393216

commit v6 on v5

--- a/solution.py
+++ b/solution.py
@@ -248,12 +248,10 @@
                 owned.at[j, part, me], slot_sem,
             ).start()
     loads = [
-        pltpu.make_async_copy(source, target, load_sem.at[place])
-        for place, (source, target) in enumerate(
-            (
-                (text_hbm, text_ref), (query_gain_hbm, query_gain_ref),
-                (key_gain_hbm, key_gain_ref), (gate_hbm, gate_ref), (hidden_hbm, hidden_ref),
-            )
+        pltpu.make_async_copy(source, target, load_sem)
+        for source, target in (
+            (text_hbm, text_ref), (query_gain_hbm, query_gain_ref),
+            (key_gain_hbm, key_gain_ref), (gate_hbm, gate_ref), (hidden_hbm, hidden_ref),
         )
     ]
     for copy in loads:
@@ -620,7 +618,7 @@
             pltpu.SemaphoreType.REGULAR((devices,)),
             pltpu.SemaphoreType.REGULAR,
             pltpu.SemaphoreType.REGULAR,
-            dma((5,)),
+            dma,
             dma,
             dma,
             dma,

time: 25.5 us -> 25.5 us (level)
  no operation moved by 1% of the time
where the time goes in v6:
time: 25.5 us; the launch traced here: 25.3 us
  Pallas kernels  24.7 us (97%)
  local copies, waits for them, and re-layouts  0.68 us (3%)
    pallas_call x1, Pallas kernels, fused(): pl.pallas_call(functools.partial(fused_kernel, devices), out_shape=jax.Sh...  24.7 us
    unnamed x1, local copies, waits for them, and re-layouts  0.68 us

profile of v6, /device:TPU:0, one launch (start us, length us, event | category | flops | bytes accessed | tf_op | source)
XLA Modules:
  0.0 25.3 jit_solution(17376859557851587516)
XLA Ops:
  0.0 24.7 %shard_map.91 = bf16[32,3072]{1,0:T(8,128)(2,1)S(1)} custom-call(s32[1,32]{1,0:T(1,128)} %bitcast.2, bf16[32,3072]{1,0:T(8,128)(2,1)} %query_hbm.1, bf16[32,3072]{1,0:T(8,128)(2,1)} %key_hbm.1, bf16[32,3072]{1,0:T(8,128)(2,1)} %value_hbm.1, s32[1,4]{1,0:T(1,128)} %bitcast.3, bf16[32,3072]{1,0:T(8,128)(2,1)} %hidden_hbm.1, f32[2,128]{1,0:T(2,128)} %query_gain_hbm.1, ...), custom_call_target="tpu_custom_call" | custom-call | tf_op jit(solution)/shard_map/pallas_call | solution.py:593
  24.7 0.7 %copy.11 = bf16[32,3072]{1,0:T(8,128)(2,1)} copy(bf16[32,3072]{1,0:T(8,128)(2,1)S(1)} %shard_map.91) | data formatting | bytes 393216
